TPU v7x, 128 devices: a whole 4x4x4 slice. The times are simulated.
128 devices in a mesh: doc: 8 (over z_lo, y), ctx: 16 (over x, z_hi, core).
Axes of the slice: x: 4, y: 4, z: 4 (z_hi: 2, z_lo: 2; z = z_hi * 2 + z_lo), core: 2. Of those that a mesh axis runs over, the one named last changes fastest.
Arguments:
- summary_cache: bfloat16 [8, 64, 512, 2048], P(None, 'doc', None, 'ctx'), may hold values from -4 to 4
- queries: bfloat16 [8, 4096, 4096], P('doc', 'ctx'), may hold values from -100 to 100
- section_counts: int32 [64], replicated, may hold values from 1 to 2
- summary_blocks: int32 [64, 2], replicated, may hold values from 1 to 2
Outputs:
- attended: bfloat16 [8, 4096, 4096], P('doc', 'ctx')
- relayed: bfloat16 [8, 8, 4096, 2048], P(None, 'doc', 'ctx')
All inputs are finite; a program needn't handle non-finite values.
Results may differ from a plain program's by a relative error of at most 0.0045.
Values may be sent and summed in bfloat16 or wider, within the bound.
A program may use at most 192 MiB of HBM per device.

v0:
```python
import math

import jax
import jax.numpy as jnp
from jax import lax
from jax.sharding import PartitionSpec as P

QH = 32
KVH = 8
HD = 128
BLOCK = 128
SECTIONS = 2
GROUP = 4
SUMLEN = 256


NEGATIVE = -1e30


def relay(cache_part):
    layers, documents, slot_count, feature_count = cache_part.shape
    flattened = cache_part.reshape(layers, documents * slot_count, feature_count)
    return lax.all_to_all(
        lax.all_to_all(flattened, "doc", split_axis=1, concat_axis=1, tiled=True),
        "ctx",
        split_axis=1,
        concat_axis=2,
        tiled=True,
    )


def group_validity(section_counts, summary_blocks, group_index, row_count):
    chosen = (jnp.arange(row_count) == group_index).astype(jnp.int32)
    counts_all = section_counts.reshape(row_count, row_count)
    blocks_all = summary_blocks.reshape(row_count, row_count, SECTIONS)
    counts_here = jnp.sum(counts_all * chosen[None, :], axis=1)
    blocks_here = jnp.sum(blocks_all * chosen[None, :, None], axis=1)
    live_section = jnp.arange(SECTIONS)[None, :] < counts_here[:, None]
    live_slot = jnp.arange(SUMLEN)[None, None, :] < BLOCK * blocks_here[:, :, None]
    return (live_section[:, :, None] & live_slot).reshape(row_count * SECTIONS * SUMLEN)


def attend(attn_state, key_piece, first_row, grouped_queries, query_positions, validity):
    piece_rows = key_piece.shape[0]
    block_rows = math.gcd(piece_rows, 512)
    own_last = query_positions[-1]

    def compute(state_now):
        running_max, denominator, accumulated = state_now
        key_heads = key_piece[:, : KVH * HD].reshape(block_rows, KVH, HD)
        value_heads = key_piece[:, KVH * HD :].reshape(block_rows, KVH, HD)
        scores = jnp.einsum(
            "pkgd,skd->kgps", grouped_queries, key_heads, preferred_element_type=jnp.float32
        ) * (1.0 / math.sqrt(HD))
        key_positions = first_row + jnp.arange(block_rows)
        live_keys = lax.dynamic_slice_in_dim(validity, first_row, block_rows)
        allowed = live_keys[None, :] & (key_positions[None, :] <= query_positions[:, None])
        masked = jnp.where(allowed, scores, NEGATIVE)
        newest = jnp.maximum(running_max, jnp.max(masked, axis=-1))
        weights = jnp.where(allowed, jnp.exp(masked - newest[..., None]), 0.0)
        factor = jnp.exp(running_max - newest)
        denominator = denominator * factor + jnp.sum(weights, axis=-1)
        accumulated = accumulated * factor[..., None] + jnp.einsum(
            "kgps,skd->kgpd",
            weights.astype(jnp.bfloat16),
            value_heads,
            preferred_element_type=jnp.float32,
        )
        return (newest, denominator, accumulated)

    return lax.cond(
        first_row <= own_last, compute, lambda unchanged_state: unchanged_state, attn_state
    )


def finish(attn_state, own_rows):
    running_max, denominator, accumulated = attn_state
    result = accumulated / denominator[..., None]
    return jnp.transpose(result, (2, 0, 1, 3)).reshape(1, own_rows, QH * HD).astype(jnp.bfloat16)


def local(summary_cache, queries, section_counts, summary_blocks):
    row_count = lax.axis_size("doc")
    group_index = lax.axis_index("doc")
    shard_index = lax.axis_index("ctx")
    own_rows = queries.shape[1]
    validity = group_validity(section_counts, summary_blocks, group_index, row_count)
    query_positions = shard_index * own_rows + jnp.arange(own_rows)
    grouped_queries = queries[0].reshape(own_rows, KVH, GROUP, HD)
    initial = (
        jnp.full((KVH, GROUP, own_rows), NEGATIVE, jnp.float32),
        jnp.zeros((KVH, GROUP, own_rows), jnp.float32),
        jnp.zeros((KVH, GROUP, own_rows, HD), jnp.float32),
    )
    layers, documents, slot_count, feature_count = summary_cache.shape
    grouped = lax.all_to_all(
        summary_cache[0].reshape(documents * slot_count, feature_count),
        "doc",
        split_axis=0,
        concat_axis=0,
        tiled=True,
    )
    whole_group = lax.all_gather(grouped, "ctx", axis=1, tiled=True)
    group_rows = whole_group.shape[0]
    block_span = math.gcd(group_rows, 512)
    attn_state = initial
    for offset in range(0, group_rows, block_span):
        attn_state = attend(
            attn_state,
            whole_group[offset : offset + block_span],
            offset,
            grouped_queries,
            query_positions,
            validity,
        )
    own_first = lax.dynamic_slice_in_dim(whole_group, shard_index * own_rows, own_rows, 0)
    relayed_local = jnp.concatenate([own_first[None], relay(summary_cache[1:])], axis=0)
    attended = finish(attn_state, own_rows)
    return (
        attended,
        relayed_local.reshape(relayed_local.shape[0], 1, own_rows, relayed_local.shape[2]),
    )


def solution(mesh):
    placed = (P(None, "doc", None, "ctx"), P("doc", "ctx", None), P(), P())
    return jax.shard_map(
        local,
        mesh=mesh,
        in_specs=placed,
        out_specs=(P("doc", "ctx", None), P(None, "doc", "ctx", None)),
        check_vma=False,
    )
```

profile of v0, /device:TPU:30, one launch (start us, length us, event | category | flops | bytes accessed | tf_op | source)
XLA Modules:
  0.0 554.0 jit_solution(15792600244148587157)
XLA Ops:
  7.2 1.3 slice_bitcast_fusion
  8.5 19.5 %all_to_all.35 = bf16[8,512,128]{2,1,0:T(8,128)(2,1)S(1)} all-to-all(bf16[8,512,128]{2,1,0:T(8,128)(2,1)S(1)} %slice_bitcast_fusion), channel_id=1, replica_groups=mesh['doc'=8,'ctx'=16] {'doc'}, dimensions={0} | all-to-all | bytes 2097152 | tf_op jit(solution)/shard_map/all_to_all | solution.py:96
  28.0 1.3 copy.192
  29.3 6.9 %slice.98 = bf16[7,8,512,128]{3,2,1,0:T(8,128)(2,1)} slice(bf16[8,8,512,128]{3,2,1,0:T(8,128)(2,1)} %param.20), slice={[1:8], [0:8], [0:512], [0:128]} | slice | bytes 14680064 | tf_op jit(solution)/shard_map/slice | solution.py:117
  36.2 11.3 %copy.124 = bf16[7,8,512,128]{3,0,2,1:T(8,128)(2,1)} copy(bf16[7,8,512,128]{3,2,1,0:T(8,128)(2,1)} %slice.98) | data formatting | bytes 14680064 | tf_op jit(solution)/shard_map/slice | solution.py:117
  47.6 117.2 %all_to_all.36 = bf16[7,4096,128]{2,0,1:T(8,128)(2,1)} all-to-all(bf16[7,4096,128]{2,0,1:T(8,128)(2,1)} %bitcast.283), channel_id=1, replica_groups=mesh['doc'=8,'ctx'=16] {'doc'}, dimensions={1} | all-to-all | bytes 14680064 | tf_op jit(solution)/shard_map/all_to_all | solution.py:24
  164.8 8.2 %all-to-all-start.2 = ((bf16[7,4096,128]{2,0,1:T(8,128)(2,1)}), bf16[7,4096,128]{2,0,1:T(8,128)(2,1)}, u32[]{:S(2)}, u32[]{:S(2)}) async-start(bf16[7,4096,128]{2,0,1:T(8,128)(2,1)} %all_to_all.36), calls=%async_computation.2 | async-start | bytes 16777216 | tf_op jit(solution)/shard_map/all_to_all | solution.py:23
  173.7 3.3 copy.114
  182.8 129.2 %all-to-all-done.2 = bf16[7,4096,128]{2,0,1:T(8,128)(2,1)} async-done(((bf16[7,4096,128]{2,0,1:T(8,128)(2,1)}), bf16[7,4096,128]{2,0,1:T(8,128)(2,1)}, u32[]{:S(2)}, u32[]{:S(2)}) %all-to-all-start.2) | async-done | bytes 7340064 | tf_op jit(solution)/shard_map/all_to_all | solution.py:23
  312.0 12.0 %copy.126 = bf16[7,256,16,128]{1,3,2,0:T(8,128)(2,1)} copy(bf16[7,256,16,128]{3,0,1,2:T(8,128)(2,1)} %bitcast.56) | data formatting | bytes 14680064 | tf_op jit(solution)/shard_map/all_to_all | solution.py:23
  324.0 9.0 %fusion.99 = (bf16[512,2048]{0,1:T(8,128)(2,1)}, bf16[512,2048]{0,1:T(8,128)(2,1)}, bf16[512,2048]{0,1:T(8,128)(2,1)}, bf16[512,2048]{0,1:T(8,128)(2,1)}, bf16[5...) fusion(bf16[4096,2048]{0,1:T(8,128)(2,1)} %all-gather.2.cloned.1.call-done), kind=kLoop, calls=%fused_computation.141 | loop fusion | bytes 25165824 | tf_op jit(solution)/shard_map/slice | solution.py:110
  333.0 18.0 %conditional.8 = (f32[8,4,256]{2,1,0:T(4,128)}, f32[8,4,256]{2,1,0:T(4,128)S(1)}, f32[8,4,256,128]{3,2,1,0:T(8,128)}) conditional(s32[]{:T(128)} %bitcast.47, () %tuple.59, (pred[4096]{0:T(1024)(128)(4,1)S(1)}, s32[256]{0:T(256)S(1)}, bf16[512,2048]{0,1:T(8,128)(2,1)S(1)}, bf16[256,8,4,128]{0,3,2,1:T(8,128)(2,1)S(1)}) %tuple.164), branch_computations={%region_2.0_spmd, %region_3.6_spmd} | conditional | flops 2203353088 | bytes 63801880 | solution.py:71
  333.8 2.8 fusion
  337.2 5.1 fusion.2
  342.2 0.8 fusion.12
  343.0 8.0 %broadcast_add_fusion = f32[8,4,256,128]{3,2,1,0:T(8,128)} fusion(f32[8,4,256]{2,1,0:T(4,128)S(1)} %get-tuple-element.412, bf16[512,8,128,1]{0,2,3,1:T(8,128)(2,1)S(1)} %bitcast.315, f32[8,512,256,4]{2,1,3,0:T(8,128)S(1)} %get-tuple-element.431, f32[8,4,256]{2,1,0:T(4,128)} %get-tuple-element.483, pred[256,512]{0,1:T(8,128)(4,1)S(1)} %fusion.8), kind=kOutput, calls=%fused_computation.7 | convolution fusion | flops 1095761920 | bytes 22216704 | tf_op jit(solution)/shard_map/cond/branch_1_fun/kgps,skd->kgpd/dot_general | solution.py:63
  351.0 27.5 %conditional.9 = ((f32[8,4,256]{2,1,0:T(4,128)}, f32[8,4,256]{2,1,0:T(4,128)S(1)}, f32[8,4,256,128]{3,2,1,0:T(8,128)})) conditional(s32[]{:T(128)} %bitcast.46, (f32[8,4,256]{2,1,0:T(4,128)}, f32[8,4,256]{2,1,0:T(4,128)S(1)}, f32[8,4,256,128]{3,2,1,0:T(8,128)}) %conditional.8, (pred[4096]{0:T(1024)(128)(4,1)S(1)}, s32[256]{0:T(256)S(1)}, ...), branch_computations={%region_6.7_spmd, %region_7.10_spmd} | conditional | flops 2204385792 | bytes 135273024 | solution.py:71
  351.4 1.7 fusion.92
  353.0 2.8 fusion.13
  355.8 0.8 max.14
  356.6 4.9 copy-done
  361.5 4.3 fusion.15
  366.6 11.3 %multiply_add_fusion = f32[8,4,256,128]{3,2,1,0:T(8,128)} fusion(f32[8,4,256,128]{3,2,1,0:T(8,128)} %get-tuple-element.158, f32[8,4,256]{2,1,0:T(4,128)S(1)} %bitcast.331, bf16[512,8,128,1]{0,2,3,1:T(8,128)(2,1)S(1)} %bitcast.308, f32[8,512,256,4]{2,1,3,0:T(8,128)} %copy-done, f32[8,4,256]{2,1,0:T(4,128)S(1)} %max.14, pred[256,512]{0,1:T(8,128)(4,1)S(1)} %compare_and_fusion), kind=kOutput, calls=%fused_computation.23 | convolution fusion | flops 1096810496 | bytes 26411008 | tf_op jit(solution)/shard_map/cond/branch_1_fun/kgps,skd->kgpd/dot_general | solution.py:63
  378.5 27.6 %conditional.10 = ((f32[8,4,256]{2,1,0:T(4,128)}, f32[8,4,256]{2,1,0:T(4,128)S(1)}, f32[8,4,256,128]{3,2,1,0:T(8,128)})) conditional(s32[]{:T(128)} %bitcast.45, (f32[8,4,256]{2,1,0:T(4,128)}, f32[8,4,256]{2,1,0:T(4,128)S(1)}, f32[8,4,256,128]{3,2,1,0:T(8,128)}) %get-tuple-element.526, (pred[4096]{0:T(1024)(128)(4,1)S(1)}, s32[256]{0:T(256)S(1)}, ...), branch_computations={%region_10.11_spmd, %region_11.14_spmd} | conditional | flops 2204385792 | bytes 135273024 | solution.py:71
  378.9 1.7 fusion.93
  380.6 2.8 fusion.24
  383.4 0.8 max.15
  384.2 4.9 copy-done.1
  389.1 4.3 fusion.26
  394.1 11.3 %multiply_add_fusion.2 = f32[8,4,256,128]{3,2,1,0:T(8,128)} fusion(f32[8,4,256,128]{3,2,1,0:T(8,128)} %get-tuple-element.165, f32[8,4,256]{2,1,0:T(4,128)S(1)} %bitcast.332, bf16[512,8,128,1]{0,2,3,1:T(8,128)(2,1)S(1)} %bitcast.309, f32[8,512,256,4]{2,1,3,0:T(8,128)} %copy-done.1, f32[8,4,256]{2,1,0:T(4,128)S(1)} %max.15, ...), kind=kOutput, calls=%fused_computation.38 | convolution fusion | flops 1096810496 | bytes 26411008 | tf_op jit(solution)/shard_map/cond/branch_1_fun/kgps,skd->kgpd/dot_general | solution.py:63
  406.1 27.6 %conditional.11 = ((f32[8,4,256]{2,1,0:T(4,128)}, f32[8,4,256]{2,1,0:T(4,128)S(1)}, f32[8,4,256,128]{3,2,1,0:T(8,128)})) conditional(s32[]{:T(128)} %bitcast.44, (f32[8,4,256]{2,1,0:T(4,128)}, f32[8,4,256]{2,1,0:T(4,128)S(1)}, f32[8,4,256,128]{3,2,1,0:T(8,128)}) %get-tuple-element.527, (pred[4096]{0:T(1024)(128)(4,1)S(1)}, s32[256]{0:T(256)S(1)}, ...), branch_computations={%region_14.15_spmd, %region_15.18_spmd} | conditional | flops 2204385792 | bytes 135273024 | solution.py:71
  406.6 1.7 fusion.94
  408.2 2.8 fusion.35
  411.0 0.8 max.16
  411.8 4.9 copy-done.2
  416.7 4.3 fusion.37
  421.8 11.3 %multiply_add_fusion.4 = f32[8,4,256,128]{3,2,1,0:T(8,128)} fusion(f32[8,4,256,128]{3,2,1,0:T(8,128)} %get-tuple-element.172, f32[8,4,256]{2,1,0:T(4,128)S(1)} %bitcast.333, bf16[512,8,128,1]{0,2,3,1:T(8,128)(2,1)S(1)} %bitcast.310, f32[8,512,256,4]{2,1,3,0:T(8,128)} %copy-done.2, f32[8,4,256]{2,1,0:T(4,128)S(1)} %max.16, ...), kind=kOutput, calls=%fused_computation.53 | convolution fusion | flops 1096810496 | bytes 26411008 | tf_op jit(solution)/shard_map/cond/branch_1_fun/kgps,skd->kgpd/dot_general | solution.py:63
  433.7 27.8 %conditional.12 = ((f32[8,4,256]{2,1,0:T(4,128)}, f32[8,4,256]{2,1,0:T(4,128)S(1)}, f32[8,4,256,128]{3,2,1,0:T(8,128)})) conditional(s32[]{:T(128)} %bitcast.43, (f32[8,4,256]{2,1,0:T(4,128)}, f32[8,4,256]{2,1,0:T(4,128)S(1)}, f32[8,4,256,128]{3,2,1,0:T(8,128)}) %get-tuple-element.528, (pred[4096]{0:T(1024)(128)(4,1)S(1)}, s32[256]{0:T(256)S(1)}, ...), branch_computations={%region_18.19_spmd, %region_19.22_spmd} | conditional | flops 2204385792 | bytes 135273024 | solution.py:71
  434.4 1.7 fusion.95
  436.1 2.8 fusion.46
  438.8 0.8 max.17
  439.6 4.9 copy-done.3
  444.5 4.3 fusion.48
  449.6 11.3 %multiply_add_fusion.6 = f32[8,4,256,128]{3,2,1,0:T(8,128)} fusion(f32[8,4,256,128]{3,2,1,0:T(8,128)} %get-tuple-element.179, f32[8,4,256]{2,1,0:T(4,128)S(1)} %bitcast.334, bf16[512,8,128,1]{0,2,3,1:T(8,128)(2,1)S(1)} %bitcast.311, f32[8,512,256,4]{2,1,3,0:T(8,128)} %copy-done.3, f32[8,4,256]{2,1,0:T(4,128)S(1)} %max.17, ...), kind=kOutput, calls=%fused_computation.68 | convolution fusion | flops 1096810496 | bytes 26411008 | tf_op jit(solution)/shard_map/cond/branch_1_fun/kgps,skd->kgpd/dot_general | solution.py:63
  461.5 27.5 %conditional.13 = ((f32[8,4,256]{2,1,0:T(4,128)}, f32[8,4,256]{2,1,0:T(4,128)S(1)}, f32[8,4,256,128]{3,2,1,0:T(8,128)})) conditional(s32[]{:T(128)} %bitcast.42, (f32[8,4,256]{2,1,0:T(4,128)}, f32[8,4,256]{2,1,0:T(4,128)S(1)}, f32[8,4,256,128]{3,2,1,0:T(8,128)}) %get-tuple-element.529, (pred[4096]{0:T(1024)(128)(4,1)S(1)}, s32[256]{0:T(256)S(1)}, ...), branch_computations={%region_22.23_spmd, %region_23.26_spmd} | conditional | flops 2204385792 | bytes 135273024 | solution.py:71
  461.9 1.7 fusion.96
  463.6 2.8 fusion.57
  466.4 0.8 max.18
  467.2 4.9 copy-done.4
  472.1 4.3 fusion.59
  477.1 11.3 %multiply_add_fusion.8 = f32[8,4,256,128]{3,2,1,0:T(8,128)} fusion(f32[8,4,256,128]{3,2,1,0:T(8,128)} %get-tuple-element.186, f32[8,4,256]{2,1,0:T(4,128)S(1)} %bitcast.335, bf16[512,8,128,1]{0,2,3,1:T(8,128)(2,1)S(1)} %bitcast.312, f32[8,512,256,4]{2,1,3,0:T(8,128)} %copy-done.4, f32[8,4,256]{2,1,0:T(4,128)S(1)} %max.18, ...), kind=kOutput, calls=%fused_computation.83 | convolution fusion | flops 1096810496 | bytes 26411008 | tf_op jit(solution)/shard_map/cond/branch_1_fun/kgps,skd->kgpd/dot_general | solution.py:63
  489.1 27.6 %conditional.14 = ((f32[8,4,256]{2,1,0:T(4,128)}, f32[8,4,256]{2,1,0:T(4,128)S(1)}, f32[8,4,256,128]{3,2,1,0:T(8,128)})) conditional(s32[]{:T(128)} %bitcast.41, (f32[8,4,256]{2,1,0:T(4,128)}, f32[8,4,256]{2,1,0:T(4,128)S(1)}, f32[8,4,256,128]{3,2,1,0:T(8,128)}) %get-tuple-element.530, (pred[4096]{0:T(1024)(128)(4,1)S(1)}, s32[256]{0:T(256)S(1)}, ...), branch_computations={%region_26.27_spmd, %region_27.30_spmd} | conditional | flops 2204385792 | bytes 135273024 | solution.py:71
  489.5 1.7 fusion.97
  491.2 2.8 fusion.68
  494.0 0.8 max.19
  494.8 4.9 copy-done.5
  499.7 4.3 fusion.70
  504.7 11.3 %multiply_add_fusion.10 = f32[8,4,256,128]{3,2,1,0:T(8,128)} fusion(f32[8,4,256,128]{3,2,1,0:T(8,128)} %get-tuple-element.193, f32[8,4,256]{2,1,0:T(4,128)S(1)} %bitcast.336, bf16[512,8,128,1]{0,2,3,1:T(8,128)(2,1)S(1)} %bitcast.313, f32[8,512,256,4]{2,1,3,0:T(8,128)} %copy-done.5, f32[8,4,256]{2,1,0:T(4,128)S(1)} %max.19, ...), kind=kOutput, calls=%fused_computation.98 | convolution fusion | flops 1096810496 | bytes 26411008 | tf_op jit(solution)/shard_map/cond/branch_1_fun/kgps,skd->kgpd/dot_general | solution.py:63
  516.9 2.9 fusion.90
  519.8 3.0 copy.123
  522.7 4.5 convert_element_type.119
  527.2 1.3 dynamic-slice_bitcast_fusion
  528.5 7.0 %maximum_bitcast_fusion = bf16[8,1,256,2048]{2,3,0,1:T(8,128)(2,1)} fusion(bf16[7,256,2048]{1,2,0:T(8,128)(2,1)} %bitcast.284, bf16[1,256,2048]{1,2,0:T(8,128)(2,1)S(1)} %dynamic-slice_bitcast_fusion), kind=kLoop, calls=%fused_computation.121 | loop fusion | flops 4194304 | bytes 16777216 | tf_op jit(solution)/shard_map/reshape | solution.py:121
  535.5 11.4 %copy.127 = bf16[8,1,256,2048]{3,2,1,0:T(8,128)(2,1)} copy(bf16[8,1,256,2048]{2,3,0,1:T(8,128)(2,1)} %maximum_bitcast_fusion) | data formatting | bytes 16777216
  (60 shorter events, 12.1 us)
Async XLA Ops:
  7.2 316.8 %all-gather.2.cloned.1.call-start = ((), (), s32[]{:S(2)}) async-start(), calls=%async_computation.3 | async-start | bytes 17825792 | tf_op jit(solution)/shard_map/all_gather | solution.py:103
  47.6 125.4 %copy-start.7 = (s32[64,2]{0,1:T(2,128)S(1)}, s32[64,2]{0,1:T(2,128)}, u32[]{:S(2)}) copy-start(s32[64,2]{0,1:T(2,128)} %param.23) | copy-start | bytes 1540
  47.6 125.7 %copy-start.8 = (s32[64]{0:T(128)S(1)}, s32[64]{0:T(128)}, u32[]{:S(2)}) copy-start(s32[64]{0:T(128)} %param.22) | copy-start | bytes 772
  164.8 147.2 %all-to-all-start.2 = ((bf16[7,4096,128]{2,0,1:T(8,128)(2,1)}), bf16[7,4096,128]{2,0,1:T(8,128)(2,1)}, u32[]{:S(2)}, u32[]{:S(2)}) async-start(bf16[7,4096,128]{2,0,1:T(8,128)(2,1)} %all_to_all.36), calls=%async_computation.2 | async-start | bytes 16777216 | tf_op jit(solution)/shard_map/all_to_all | solution.py:23
  355.8 5.7 %copy-start = (f32[8,512,256,4]{2,1,3,0:T(8,128)}, f32[8,512,256,4]{2,1,3,0:T(8,128)S(1)}, u32[]{:S(2)}) copy-start(f32[8,512,256,4]{2,1,3,0:T(8,128)S(1)} %get-tuple-element.435) | copy-start | bytes 50331652 | tf_op jit(solution)/shard_map/cond
  383.4 5.7 %copy-start.1 = (f32[8,512,256,4]{2,1,3,0:T(8,128)}, f32[8,512,256,4]{2,1,3,0:T(8,128)S(1)}, u32[]{:S(2)}) copy-start(f32[8,512,256,4]{2,1,3,0:T(8,128)S(1)} %get-tuple-element.439) | copy-start | bytes 50331652 | tf_op jit(solution)/shard_map/cond
  411.0 5.7 %copy-start.2 = (f32[8,512,256,4]{2,1,3,0:T(8,128)}, f32[8,512,256,4]{2,1,3,0:T(8,128)S(1)}, u32[]{:S(2)}) copy-start(f32[8,512,256,4]{2,1,3,0:T(8,128)S(1)} %get-tuple-element.443) | copy-start | bytes 50331652 | tf_op jit(solution)/shard_map/cond
  438.8 5.7 %copy-start.3 = (f32[8,512,256,4]{2,1,3,0:T(8,128)}, f32[8,512,256,4]{2,1,3,0:T(8,128)S(1)}, u32[]{:S(2)}) copy-start(f32[8,512,256,4]{2,1,3,0:T(8,128)S(1)} %get-tuple-element.447) | copy-start | bytes 50331652 | tf_op jit(solution)/shard_map/cond
  466.4 5.7 %copy-start.4 = (f32[8,512,256,4]{2,1,3,0:T(8,128)}, f32[8,512,256,4]{2,1,3,0:T(8,128)S(1)}, u32[]{:S(2)}) copy-start(f32[8,512,256,4]{2,1,3,0:T(8,128)S(1)} %get-tuple-element.451) | copy-start | bytes 50331652 | tf_op jit(solution)/shard_map/cond
  493.9 5.7 %copy-start.5 = (f32[8,512,256,4]{2,1,3,0:T(8,128)}, f32[8,512,256,4]{2,1,3,0:T(8,128)S(1)}, u32[]{:S(2)}) copy-start(f32[8,512,256,4]{2,1,3,0:T(8,128)S(1)} %get-tuple-element.455) | copy-start | bytes 50331652 | tf_op jit(solution)/shard_map/cond
Sparse Core Ops, SparseCore 0:
  29.5 278.6 all-gather.1
where the time goes:
time: 563 us; the launch traced here: 554 us
  blocking collectives  137 us (24%)
  waiting for transfers between devices  129 us (23%)
  local copies, waits for them, and re-layouts  109 us (19%)
  matrix products  95.2 us (17%)
  other arithmetic  53.2 us (9%)
  between operations  19.6 us (3%)
  starting transfers between devices  8.25 us (1%)
    all_to_all x1, waiting for transfers between devices, relay(): lax.all_to_all(lax.all_to_all(flattened, 'doc', split_axis=1, concat_axis...  129 us
    all_to_all x1, blocking collectives, relay(): lax.all_to_all(flattened, 'doc', split_axis=1, concat_axis=1, tiled=True)  117 us
    dot_general x7, matrix products, compute(): jnp.einsum('kgps,skd->kgpd', weights.astype(jnp.bfloat16), value_heads, p...  75.9 us
    cond x18, local copies, waits for them, and re-layouts  33.1 us
    reduce_sum x7, other arithmetic, compute(): denominator = denominator * factor + jnp.sum(weights, axis=-1)  30.6 us
    all_to_all x1, blocking collectives, local(): lax.all_to_all(summary_cache[0].reshape(documents * slot_count, feature_c...  19.5 us
    dot_general x7, matrix products, compute(): jnp.einsum('pkgd,skd->kgps', grouped_queries, key_heads, preferred_elemen...  19.3 us
    slice x2, local copies, waits for them, and re-layouts, local(): summary_cache[1:]  18.2 us
  transfers between devices with their start and end apart: 2, of which 1 were waited for; matrix products, arithmetic and copies ran while one was open for 6% of the time, Pallas kernels for 0%

commit v1 on v0

v1 whole, which is shorter than its diff:
```python
import functools
import math

import jax
import jax.numpy as jnp
from jax import lax
from jax.experimental import pallas as pl
from jax.experimental.pallas import tpu as pltpu
from jax.sharding import PartitionSpec as P

QH = 32
KVH = 8
HD = 128
BLOCK = 128
SECTIONS = 2
GROUP = 4
SUMLEN = 256
SEQD = 512
LAYERS = 8
GSEQ = 4096
CHUNKS = 16
NEGATIVE = -1e30
MESH = pl.DeviceIdType.MESH
SCALE = (1.0 / math.sqrt(HD)) * math.log2(math.e)


def place(x, y, z, core):
    return (lax.rem(z, 2) * 4 + y, x * 4 + (z // 2) * 2 + core)


def relay_kernel(cache, out, keys, ybuf, z0, zbuf, ysend, yrecv, yown, zsend, zrecv, xsend, xrecv, xown, gsend, grecv, gown, fsend, frecv, oown):
    d = lax.axis_index("doc")
    c = lax.axis_index("ctx")
    zl, y = d // 4, lax.rem(d, 4)
    x, zh, core = c // 4, lax.rem(c // 2, 2), lax.rem(c, 2)
    z = zh * 2 + zl
    chunk = zh * 2 + core
    doc_here = x * 2 + zh
    sibling = place(x, y, z, 1 - core)

    def remote(src, dst, ssem, rsem, dev):
        return pltpu.make_async_remote_copy(src, dst, ssem, rsem, device_id=dev, device_id_type=MESH)

    def y_copy(layer, step):
        to = lax.rem(y + step, 4)
        return remote(cache.at[layer, :, to], ybuf.at[layer, y], ysend.at[layer, step - 1], yrecv.at[layer, step - 1], place(x, to, z, core))

    def y_keep(layer):
        return pltpu.make_async_copy(cache.at[layer, :, y], ybuf.at[layer, y], yown.at[layer])

    @pl.loop(0, LAYERS)
    def _(layer):
        for step in (1, 3, 2):
            y_copy(layer, step).start()
        y_keep(layer).start()

    def wait_y(layer):
        for step in (1, 2, 3):
            y_copy(layer, step).wait_recv()
        y_keep(layer).wait()

    def g_z(step, flip):
        to_z, to_core = lax.rem(z + step, 4), lax.rem(core + flip, 2)
        src = ybuf.at[0, :, lax.rem(to_z, 2), to_core]
        dst = z0.at[chunk, pl.ds(zl * 4, 4)]
        r = step * 2 + flip
        if r == 0:
            return pltpu.make_async_copy(src, dst, zrecv.at[0, 0])
        return remote(src, dst, zsend.at[0, r], zrecv.at[0, r], place(x, y, to_z, to_core))

    wait_y(0)
    for step, flip in ((1, 0), (1, 1), (3, 0), (3, 1), (2, 0), (2, 1), (0, 1), (0, 0)):
        g_z(step, flip).start()
    for r in range(8):
        if r == 0:
            g_z(0, 0).wait()
        else:
            g_z(r // 2, r % 2).wait_recv()

    def g_x(piece, step, to, docs):
        src = z0.at[piece, pl.ds(0, docs)]
        dst = keys.at[x * 4 + piece, pl.ds(0, docs), core]
        return remote(src, dst, gsend.at[piece, step - 1], grecv.at[piece, step - 1], place(to, y, z, core))

    for piece in range(4):
        for step in (1, 3, 2):
            to = lax.rem(x + step, 4)
            for v in range(4):
                @pl.when(to == v)
                def _():
                    g_x(piece, step, to, 2 * (v + 1)).start()

    def g_own(piece, docs):
        return pltpu.make_async_copy(z0.at[piece, pl.ds(0, docs)], keys.at[x * 4 + piece, pl.ds(0, docs), core], gown.at[piece])

    def g_f(piece, step, docs):
        frm = lax.rem(x - step + 4, 4)
        dst = keys.at[frm * 4 + piece, pl.ds(0, docs), core]
        src = z0.at[piece, pl.ds(0, docs)] if step == 0 else dst
        return remote(src, dst, fsend.at[piece, step], frecv.at[piece, step], sibling)

    def own_row(piece, step):
        frm = lax.rem(x - step + 4, 4)
        cols = pl.ds(pl.multiple_of((frm * 4 + piece) * HD, HD), HD)
        src = z0.at[piece, doc_here] if step == 0 else keys.at[frm * 4 + piece, doc_here, core]
        return pltpu.make_async_copy(src, out.at[0, :, cols], oown.at[piece, step])

    def each_x(body):
        for v in range(4):
            @pl.when(x == v)
            def _():
                body(2 * (v + 1))

    def first(docs):
        for piece in range(4):
            g_own(piece, docs).start()
            g_f(piece, 0, docs).start()

    each_x(first)
    for piece in range(4):
        own_row(piece, 0).start()

    def z_copy(layer, step, flip):
        to_z, to_core = lax.rem(z + step, 4), lax.rem(core + flip, 2)
        r = step * 2 + flip
        src = ybuf.at[layer, pl.ds(to_z // 2, 2, 2), lax.rem(to_z, 2), to_core]
        dst = zbuf.at[layer - 1, pl.ds(zl * 2, 2), chunk]
        return src, dst, to_z, to_core, r

    def z_one(layer, step, flip, hi):
        to_z, to_core = lax.rem(z + step, 4), lax.rem(core + flip, 2)
        r = step * 2 + flip
        src = ybuf.at[layer, hi * 2 + to_z // 2, lax.rem(to_z, 2), to_core]
        dst = zbuf.at[layer - 1, zl * 2 + hi, chunk]
        if r == 0:
            return pltpu.make_async_copy(src, dst, zrecv.at[layer, hi * 8])
        return remote(src, dst, zsend.at[layer, hi * 8 + r], zrecv.at[layer, hi * 8 + r], place(x, y, to_z, to_core))

    def x_copy(layer, step, piece):
        to = lax.rem(x + step, 4)
        cols = pl.ds(pl.multiple_of((x * 4 + piece) * HD, HD), HD)
        src = zbuf.at[layer - 1, to, piece]
        dst = out.at[layer, :, cols]
        if step == 0:
            return pltpu.make_async_copy(src, dst, xown.at[layer - 1, piece])
        return remote(src, dst, xsend.at[layer - 1, step - 1, piece], xrecv.at[layer - 1, step - 1, piece], place(to, y, z, core))

    def pass_on(piece):
        def body(docs):
            for step in (1, 3, 2):
                g_x(piece, step, x, docs).wait_recv()
                g_f(piece, step, docs).start()
        each_x(body)
        for step in (1, 3, 2):
            own_row(piece, step).start()

    @pl.loop(1, LAYERS)
    def _(layer):
        wait_y(layer)
        for step, flip in ((1, 0), (1, 1), (3, 0), (3, 1), (2, 0), (2, 1), (0, 1), (0, 0)):
            for hi in range(2):
                z_one(layer, step, flip, hi).start()
        for r in range(8):
            for hi in range(2):
                if r == 0:
                    z_one(layer, 0, 0, hi).wait()
                else:
                    z_one(layer, r // 2, r % 2, hi).wait_recv()
        for step in (1, 3, 2, 0):
            for piece in range(4):
                x_copy(layer, step, piece).start()

    for piece in range(4):
        pass_on(piece)

    def drain(docs):
        for piece in range(4):
            g_own(piece, docs).wait()
            for step in range(4):
                g_f(piece, step, docs).wait()

    each_x(drain)
    for piece in range(4):
        for step in (1, 3, 2):
            to = lax.rem(x + step, 4)
            for v in range(4):
                @pl.when(to == v)
                def _():
                    g_x(piece, step, to, 2 * (v + 1)).wait_send()
        for step in range(4):
            own_row(piece, step).wait()
    for r in range(1, 8):
        g_z(r // 2, r % 2).wait_send()
    for step in (1, 2, 3):
        y_copy(0, step).wait_send()

    @pl.loop(1, LAYERS)
    def _(layer):
        for step in (1, 2, 3):
            y_copy(layer, step).wait_send()
        for r in range(1, 8):
            for hi in range(2):
                z_one(layer, r // 2, r % 2, hi).wait_send()
        for piece in range(4):
            x_copy(layer, 0, piece).wait()
            for step in (1, 2, 3):
                x_copy(layer, step, piece).wait()


def relay(cache):
    dma = pltpu.SemaphoreType.DMA
    bf = jnp.bfloat16
    anyspace = pl.BlockSpec(memory_space=pl.ANY)
    return pl.pallas_call(
        relay_kernel,
        out_shape=(
            jax.ShapeDtypeStruct((LAYERS, 256, 2048), bf),
            jax.ShapeDtypeStruct((CHUNKS, 8, 2, 256, HD), bf),
            jax.ShapeDtypeStruct((LAYERS, 4, 2, 2, 256, HD), bf),
        ),
        in_specs=[anyspace],
        out_specs=(anyspace,) * 3,
        scratch_shapes=[
            pltpu.VMEM((4, 8, 256, HD), bf),
            pltpu.VMEM((LAYERS - 1, 4, 4, 256, HD), bf),
            dma((8, 3)), dma((8, 3)), dma((8,)),
            dma((8, 16)), dma((8, 16)),
            dma((7, 3, 4)), dma((7, 3, 4)), dma((7, 4)),
            dma((4, 3)), dma((4, 3)), dma((4,)),
            dma((4, 4)), dma((4, 4)), dma((4, 4)),
        ],
        compiler_params=pltpu.CompilerParams(has_side_effects=True, vmem_limit_bytes=40 << 20),
    )(cache.reshape(LAYERS, 2, 4, 2, 256, HD))


def attend_kernel(q_ref, k_ref, v_ref, bias_ref, o_ref, m_ref, l_ref, acc_ref):
    c = lax.axis_index("ctx")
    mine = c // 2
    half = lax.rem(c, 2)
    q = jnp.concatenate([q_ref[:, g * HD : (g + 1) * HD] for g in range(GROUP)], axis=0)
    rows = q.shape[0]

    def step(doc, diagonal, first):
        k = k_ref[0, pl.ds(pl.multiple_of(doc * SEQD, SEQD), SEQD), :]
        v = v_ref[0, pl.ds(pl.multiple_of(doc * SEQD, SEQD), SEQD), :]
        s = lax.dot_general(q, k, (((1,), (1,)), ((), ())), preferred_element_type=jnp.float32)
        s = s * SCALE + bias_ref[pl.ds(doc, 1), :]
        if diagonal:
            at = lax.rem(lax.broadcasted_iota(jnp.int32, s.shape, 0), 256) + half * 256
            s = jnp.where(lax.broadcasted_iota(jnp.int32, s.shape, 1) <= at, s, NEGATIVE)
        top = m_ref[...]
        newest = jnp.maximum(top, jnp.max(s, axis=1, keepdims=True))
        w = jnp.exp2(s - newest)
        factor = jnp.exp2(top - newest)
        m_ref[...] = newest
        part = w[:, 0:128] + w[:, 128:256] + w[:, 256:384] + w[:, 384:512]
        l_ref[...] = l_ref[...] * factor + part
        acc_ref[...] = acc_ref[...] * factor + lax.dot_general(
            w.astype(jnp.bfloat16), v, (((1,), (0,)), ((), ())), preferred_element_type=jnp.float32
        )

    m_ref[...] = jnp.full(m_ref.shape, NEGATIVE, jnp.float32)
    l_ref[...] = jnp.zeros_like(l_ref)
    acc_ref[...] = jnp.zeros_like(acc_ref)

    @pl.loop(0, mine)
    def _(doc):
        step(doc, False, False)

    step(mine, True, False)
    result = (acc_ref[...] / jnp.sum(l_ref[...], axis=1, keepdims=True)).astype(jnp.bfloat16)
    for g in range(GROUP):
        o_ref[:, g * HD : (g + 1) * HD] = result[g * 256 : (g + 1) * 256]


def attention(queries, keys, bias):
    return pl.pallas_call(
        attend_kernel,
        grid=(KVH,),
        out_shape=jax.ShapeDtypeStruct((256, QH * HD), jnp.bfloat16),
        in_specs=[
            pl.BlockSpec((256, GROUP * HD), lambda k: (0, k)),
            pl.BlockSpec((1, GSEQ, HD), lambda k: (k, 0, 0)),
            pl.BlockSpec((1, GSEQ, HD), lambda k: (k + KVH, 0, 0)),
            pl.BlockSpec((8, SEQD), lambda k: (0, 0)),
        ],
        out_specs=pl.BlockSpec((256, GROUP * HD), lambda k: (0, k)),
        scratch_shapes=[
            pltpu.VMEM((GROUP * 256, 1), jnp.float32),
            pltpu.VMEM((GROUP * 256, 128), jnp.float32),
            pltpu.VMEM((GROUP * 256, HD), jnp.float32),
        ],
        compiler_params=pltpu.CompilerParams(vmem_limit_bytes=40 << 20),
    )(queries, keys, keys, bias)


def key_bias(section_counts, summary_blocks):
    chosen = (jnp.arange(8) == lax.axis_index("doc")).astype(jnp.int32)
    counts = jnp.sum(section_counts.reshape(8, 8) * chosen[None, :], axis=1)
    blocks = jnp.sum(summary_blocks.reshape(8, 8, SECTIONS) * chosen[None, :, None], axis=1)
    live_section = jnp.arange(SECTIONS)[None, :] < counts[:, None]
    live_slot = jnp.arange(SUMLEN)[None, None, :] < BLOCK * blocks[:, :, None]
    live = (live_section[:, :, None] & live_slot).reshape(8, SEQD)
    return jnp.where(live, 0.0, NEGATIVE).astype(jnp.float32)


def local(summary_cache, queries, section_counts, summary_blocks):
    bias = key_bias(section_counts, summary_blocks)
    relayed, keys, _ = relay(summary_cache)
    attended = attention(queries[0], keys.reshape(CHUNKS, GSEQ, HD), bias)
    return attended[None], relayed[:, None]


def solution(mesh):
    placed = (P(None, "doc", None, "ctx"), P("doc", "ctx", None), P(), P())
    return jax.shard_map(
        local,
        mesh=mesh,
        in_specs=placed,
        out_specs=(P("doc", "ctx", None), P(None, "doc", "ctx", None)),
        check_vma=False,
    )
```

time: 563 us -> 367 us (0.65)
  the two profiles are of different devices: /device:TPU:30 before, /device:TPU:103 now
where the time goes in v1:
time: 367 us; the launch traced here: 366 us
  Pallas kernels  353 us (96%)
  local copies, waits for them, and re-layouts  12 us (3%)
    pallas_call x1, Pallas kernels, relay(): pl.pallas_call(relay_kernel, out_shape=(jax.ShapeDtypeStruct((LAYERS, 256...  223 us
    pallas_call x1, Pallas kernels, attention(): pl.pallas_call(attend_kernel, grid=(KVH,), out_shape=jax.ShapeDtypeStruct...  130 us
    unnamed x11, local copies, waits for them, and re-layouts  11.7 us

profile of v1, /device:TPU:103, one launch (start us, length us, event | category | flops | bytes accessed | tf_op | source)
XLA Modules:
  0.0 366.3 jit_solution(16027905864488932452)
XLA Ops:
  0.6 0.0 copy-start.1
  0.6 0.0 copy-start.3
  0.7 0.0 copy-start.2
  0.7 222.8 %shard_map.59 = (bf16[8,256,2048]{2,1,0:T(8,128)(2,1)S(1)}, bf16[16,8,2,256,128]{4,3,2,1,0:T(8,128)(2,1)}, bf16[8,4,2,2,256,128]{5,4,3,2,1,0:T(8,128)(2,1)}) custom-call(bf16[8,2,4,2,256,128]{5,4,3,2,1,0:T(8,128)(2,1)} %bitcast.18), custom_call_target="tpu_custom_call" | custom-call | tf_op jit(solution)/shard_map/pallas_call | solution.py:214
  223.5 0.0 copy-start
  223.5 3.2 copy-done
  226.7 0.0 copy-done.3
  226.7 0.1 reshape.57
  226.8 0.1 multiply_reduce_fusion.1
  226.9 0.1 and.12
  227.0 0.0 copy-done.2
  227.0 0.1 reshape.58
  227.1 0.2 multiply_reduce_fusion
  227.2 0.1 lt.43
  227.3 0.0 copy-done.1
  227.3 130.5 %shard_map.60 = bf16[256,4096]{1,0:T(8,128)(2,1)} custom-call(bf16[256,4096]{1,0:T(8,128)(2,1)S(1)} %bitcast.15, bf16[16,4096,128]{2,1,0:T(8,128)(2,1)} %bitcast.16, bf16[16,4096,128]{2,1,0:T(8,128)(2,1)} %bitcast.17, f32[8,512]{1,0:T(8,128)S(1)} %and_select_fusion.bias_ref), custom_call_target="tpu_custom_call" | custom-call | tf_op jit(solution)/shard_map/pallas_call | solution.py:277
  357.8 8.4 %copy.9 = bf16[8,1,256,2048]{3,2,1,0:T(8,128)(2,1)} copy(bf16[8,1,256,2048]{3,2,1,0:T(8,128)(2,1)} %bitcast.14) | data formatting | bytes 16777216
  (6 shorter events, 0.0 us)
Async XLA Ops:
  0.6 226.7 %copy-start.1 = (bf16[1,256,4096]{2,1,0:T(8,128)(2,1)S(1)}, bf16[1,256,4096]{2,1,0:T(8,128)(2,1)}, u32[]{:S(2)}) copy-start(bf16[1,256,4096]{2,1,0:T(8,128)(2,1)} %param.5) | copy-start | bytes 6291460
  0.6 226.1 %copy-start.3 = (s32[64]{0:T(128)S(1)}, s32[64]{0:T(128)}, u32[]{:S(2)}) copy-start(s32[64]{0:T(128)} %param.6) | copy-start | bytes 772
  0.7 226.3 %copy-start.2 = (s32[64,2]{0,1:T(2,128)S(1)}, s32[64,2]{0,1:T(2,128)}, u32[]{:S(2)}) copy-start(s32[64,2]{0,1:T(2,128)} %param.7) | copy-start | bytes 1540
  223.5 3.2 copy-start

commit v2 on v0

v2 whole, which is shorter than its diff:
```python
import functools
import math

import jax
import jax.numpy as jnp
from jax import lax
from jax.experimental import pallas as pl
from jax.experimental.pallas import tpu as pltpu
from jax.sharding import PartitionSpec as P

QH = 32
KVH = 8
HD = 128
BLOCK = 128
SECTIONS = 2
GROUP = 4
SUMLEN = 256
SEQD = 512
LAYERS = 8
GSEQ = 4096
CHUNKS = 16
NEGATIVE = -1e30
MESH = pl.DeviceIdType.MESH
SCALE = (1.0 / math.sqrt(HD)) * math.log2(math.e)


def place(x, y, z, core):
    return (lax.rem(z, 2) * 4 + y, x * 4 + (z // 2) * 2 + core)


def head_group(mine, half, q_ref, k_ref, v_ref, bias_ref, s_ref, m_ref, l_ref, acc_ref):
    rows = q_ref.shape[0]

    def score(doc, diagonal):
        k = k_ref[doc // 2, lax.rem(doc, 2)]
        s = lax.dot_general(q_ref[...], k, (((1,), (1,)), ((), ())), preferred_element_type=jnp.float32)
        s = s * SCALE + bias_ref[pl.ds(doc, 1), :]
        if diagonal:
            at = lax.rem(lax.broadcasted_iota(jnp.int32, s.shape, 0), 256) + half * 256
            s = jnp.where(lax.broadcasted_iota(jnp.int32, s.shape, 1) <= at, s, NEGATIVE)
        s_ref[doc] = s
        top = jnp.maximum(jnp.maximum(s[:, 0:128], s[:, 128:256]), jnp.maximum(s[:, 256:384], s[:, 384:512]))
        return top

    def weigh(doc):
        v = v_ref[doc // 2, lax.rem(doc, 2)]
        top = m_ref[...]
        w = [jnp.exp2(s_ref[doc, :, i * 128 : (i + 1) * 128] - top) for i in range(4)]
        part = (w[0] + w[1]) + (w[2] + w[3])
        pair = [jnp.concatenate([w[2 * i].astype(jnp.bfloat16), w[2 * i + 1].astype(jnp.bfloat16)], axis=1) for i in range(2)]
        summed = lax.dot_general(
            jnp.concatenate(pair, axis=1), v, (((1,), (0,)), ((), ())), preferred_element_type=jnp.float32
        )
        return part, summed

    m_ref[...] = score(mine, True)

    @pl.loop(0, mine)
    def _(doc):
        m_ref[...] = jnp.maximum(m_ref[...], score(doc, False))

    m_ref[...] = jnp.broadcast_to(jnp.max(m_ref[...], axis=1, keepdims=True), m_ref.shape)
    part, summed = weigh(mine)
    l_ref[...] = part
    acc_ref[...] = summed

    @pl.loop(0, mine)
    def _(doc):
        part, summed = weigh(doc)
        l_ref[...] += part
        acc_ref[...] += summed

    return (acc_ref[...] / jnp.sum(l_ref[...], axis=1, keepdims=True)).astype(jnp.bfloat16)


ROUNDS = 4
PART = 256 // ROUNDS


def relay_kernel(
    cache, queries, bias, out, attended, keys, ybuf, z0, zbuf, kbuf, vbuf, qbuf, obuf, s_ref, m_ref, l_ref, acc_ref,
    y0s, y0r, y0o, ys, yr, yo, z0s, z0r, zs, zr, gs, gr, go, fs, fr, es, er, hs, hr, xs, xr, xo, oo, ks, vs, qs, os,
):
    d = lax.axis_index("doc")
    c = lax.axis_index("ctx")
    zl, y = d // 4, lax.rem(d, 4)
    x, zh, core = c // 4, lax.rem(c // 2, 2), lax.rem(c, 2)
    z = zh * 2 + zl
    chunk = zh * 2 + core
    sibling = place(x, y, z, 1 - core)
    partner = place(x, y, lax.rem(z + 2, 4), core)
    others = (1, 3, 2)

    def remote(src, dst, ssem, rsem, dev):
        return pltpu.make_async_remote_copy(src, dst, ssem, rsem, device_id=dev, device_id_type=MESH)

    def when_is(value, options, body):
        for v in options:
            @pl.when(value == v)
            def _():
                body(v)

    def slots(half, u):
        return pl.ds(pl.multiple_of(half * 256 + u * PART, PART), PART)

    def y0_copy(u, step):
        to = lax.rem(y + step, 4)
        rows = pl.ds(pl.multiple_of(u * PART, PART), PART)
        src = cache.at[0, :, to // 2, lax.rem(to, 2), :, rows]
        dst = ybuf.at[0, y // 2, lax.rem(y, 2), :, :, rows]
        if step == 0:
            return pltpu.make_async_copy(src, dst, y0o.at[u])
        return remote(src, dst, y0s.at[u, step - 1], y0r.at[u, step - 1], place(x, to, z, core))

    def y_copy(layer, step):
        to = lax.rem(y + step, 4)
        src = cache.at[layer, :, to // 2, lax.rem(to, 2)]
        dst = ybuf.at[layer, y // 2, lax.rem(y, 2)]
        if step == 0:
            return pltpu.make_async_copy(src, dst, yo.at[layer - 1])
        return remote(src, dst, ys.at[layer - 1, step - 1], yr.at[layer - 1, step - 1], place(x, to, z, core))

    def z0_copy(u, step, flip, both):
        to_z, to_core = lax.rem(z + step, 4), lax.rem(core + flip, 2)
        rows = pl.ds(pl.multiple_of(u * PART, PART), PART)
        r = step * 2 + flip
        if both:
            src = ybuf.at[0, :, :, lax.rem(to_z, 2), to_core, rows]
            dst = z0.at[chunk, pl.ds(zl * 2, 2), :, rows]
        else:
            src = ybuf.at[0, :, to_z // 2, lax.rem(to_z, 2), to_core, rows]
            dst = z0.at[chunk, pl.ds(zl * 2, 2), to_z // 2, rows]
        if r == 0:
            return pltpu.make_async_copy(src, dst, z0r.at[u, 0])
        return remote(src, dst, z0s.at[u, r], z0r.at[u, r], place(x, y, to_z, to_core))

    zorder = ((1, 0), (1, 1), (3, 0), (3, 1), (2, 0), (2, 1), (0, 1), (0, 0))

    def z0_send(u):
        for step in (1, 2, 3):
            y0_copy(u, step).wait_recv()
        y0_copy(u, 0).wait()

        def go_on(v):
            for step, flip in zorder:
                z0_copy(u, step, flip, v == 1).start()

        when_is(core, (0, 1), go_on)

    def z0_wait(u):
        def take(v):
            for step, flip in zorder:
                copy = z0_copy(u, step, flip, (v + flip) % 2 == 1)
                if step * 2 + flip == 0:
                    copy.wait()
                else:
                    copy.wait_recv()

        when_is(core, (0, 1), take)

    def span(ref, lead, piece, n, par, rows):
        if piece % 2:
            return ref.at[lead, pl.ds(0, n), :, rows]
        return ref.at[lead, pl.ds(0, n), par, rows]

    def near(piece, n, u):
        return span(z0, piece, piece, n, zh, pl.ds(pl.multiple_of(u * PART, PART), PART))

    def far(frm, piece, n, u):
        return span(keys, frm * 4 + piece, piece, n, zh, slots(core, u))

    def g_copy(u, piece, step, n):
        to = lax.rem(x + step, 4)
        return remote(near(piece, n, u), far(x, piece, n, u), gs.at[u, piece, step - 1], gr.at[u, piece, step - 1], place(to, y, z, core))

    def g_own(u, piece, n):
        return pltpu.make_async_copy(near(piece, n, u), far(x, piece, n, u), go.at[u, piece])

    def source(step):
        return lax.rem(x - step + 4, 4)

    def f_copy(u, piece, step, n):
        frm = source(step)
        dst = far(frm, piece, n, u)
        src = near(piece, n, u) if step == 0 else dst
        return remote(src, dst, fs.at[u, piece, step], fr.at[u, piece, step], sibling)

    def e_copy(u, piece, step, n):
        frm = source(step)
        dst = far(frm, piece, n, u)
        src = near(piece, n, u) if step == 0 else dst
        return remote(src, dst, es.at[u, piece // 2, step], er.at[u, piece // 2, step], partner)

    def h_copy(u, piece, step, n):
        here = keys.at[source(step) * 4 + piece, pl.ds(0, n), 1 - zh, slots(core, u)]
        return remote(here, here, hs.at[u, piece // 2, step], hr.at[u, piece // 2, step], sibling)

    given, taken = x + 1 - zh, x + zh

    def g_send(u):
        for step in others:
            def send(v):
                for piece in range(4):
                    g_copy(u, piece, step, v + 1).start()

            when_is(lax.rem(x + step, 4), range(4), send)

        def keep(v):
            for piece in range(4):
                f_copy(u, piece, 0, v + 1).start()
                g_own(u, piece, v + 1).start()

        when_is(x, range(4), keep)

        def swap(n):
            for piece in (0, 2):
                e_copy(u, piece, 0, n).start()

        when_is(given, range(1, 5), swap)

    def g_pass(u):
        for step in others:
            for piece in range(4):
                def take(v):
                    g_copy(u, piece, step, v + 1).wait_recv()
                    f_copy(u, piece, step, v + 1).start()

                when_is(x, range(4), take)
                if piece % 2 == 0:
                    when_is(given, range(1, 5), lambda n: e_copy(u, piece, step, n).start())

    def e_pass(u):
        def take(n):
            for step in (0,) + others:
                for piece in (0, 2):
                    e_copy(u, piece, step, n).wait_recv()
                    h_copy(u, piece, step, n).start()

        when_is(taken, range(1, 5), take)

    def own_row(piece, step):
        frm = source(step)
        cols = pl.ds(pl.multiple_of((frm * 4 + piece) * HD, HD), HD)
        if step == 0:
            src = z0.at[piece, x, zh]
        else:
            src = keys.at[frm * 4 + piece, x, zh, pl.ds(pl.multiple_of(core * 256, 256), 256)]
        return pltpu.make_async_copy(src, out.at[0, :, cols], oo.at[piece, step])

    def z_copy(layer, step, flip):
        to_z, to_core = lax.rem(z + step, 4), lax.rem(core + flip, 2)
        r = step * 2 + flip
        src = ybuf.at[layer, :, to_z // 2, lax.rem(to_z, 2), to_core]
        dst = zbuf.at[layer - 1, pl.ds(zl * 2, 2), chunk]
        if r == 0:
            return pltpu.make_async_copy(src, dst, zr.at[layer - 1, 0])
        return remote(src, dst, zs.at[layer - 1, r], zr.at[layer - 1, r], place(x, y, to_z, to_core))

    def x_copy(layer, step, piece):
        to = lax.rem(x + step, 4)
        cols = pl.ds(pl.multiple_of((x * 4 + piece) * HD, HD), HD)
        src = zbuf.at[layer - 1, to, piece]
        dst = out.at[layer, :, cols]
        if step == 0:
            return pltpu.make_async_copy(src, dst, xo.at[layer - 1, piece])
        return remote(src, dst, xs.at[layer - 1, step - 1, piece], xr.at[layer - 1, step - 1, piece], place(to, y, z, core))

    def z_send(layer):
        for step in (1, 2, 3):
            y_copy(layer, step).wait_recv()
        y_copy(layer, 0).wait()
        for step, flip in zorder:
            z_copy(layer, step, flip).start()

    def x_send(layer):
        for step, flip in zorder:
            if step * 2 + flip == 0:
                z_copy(layer, 0, 0).wait()
            else:
                z_copy(layer, step, flip).wait_recv()
        for step in (1, 3, 2, 0):
            for piece in range(4):
                x_copy(layer, step, piece).start()

    def q_copy(k, g):
        slot = lax.rem(k, 2)
        cols = pl.ds(pl.multiple_of((k * GROUP + g) * HD, HD), HD)
        return pltpu.make_async_copy(queries.at[:, cols], qbuf.at[slot, pl.ds(g * 256, 256)], qs.at[slot, g])

    def o_copy(k, g):
        slot = lax.rem(k, 2)
        cols = pl.ds(pl.multiple_of((k * GROUP + g) * HD, HD), HD)
        return pltpu.make_async_copy(obuf.at[slot, pl.ds(g * 256, 256)], attended.at[:, cols], os.at[slot, g])

    def kv_copies(k, n):
        slot = lax.rem(k, 2)
        return (
            pltpu.make_async_copy(keys.at[k, pl.ds(0, n)], kbuf.at[slot, pl.ds(0, n)], ks.at[slot]),
            pltpu.make_async_copy(keys.at[k + KVH, pl.ds(0, n)], vbuf.at[slot, pl.ds(0, n)], vs.at[slot]),
        )

    def fetch(k):
        for g in range(GROUP):
            q_copy(k, g).start()

        def body(v):
            for copy in kv_copies(k, v + 1):
                copy.start()

        when_is(x, range(4), body)

    def fetched(k):
        for g in range(GROUP):
            q_copy(k, g).wait()

        def body(v):
            for copy in kv_copies(k, v + 1):
                copy.wait()

        when_is(x, range(4), body)

    @pl.loop(0, ROUNDS)
    def _(u):
        for step in others + (0,):
            y0_copy(u, step).start()

    @pl.loop(1, LAYERS)
    def _(layer):
        for step in others + (0,):
            y_copy(layer, step).start()

    @pl.loop(0, ROUNDS + 2)
    def _(t):
        @pl.when(t < ROUNDS)
        def _():
            z0_send(t)

        @pl.when(t >= 2)
        def _():
            z0_wait(t - 2)
            g_send(t - 2)

    for piece in range(4):
        own_row(piece, 0).start()

    @pl.loop(1, LAYERS)
    def _(layer):
        z_send(layer)

        @pl.when(layer >= 2)
        def _():
            x_send(layer - 1)

        @pl.when((layer >= 2) & (layer < 2 + ROUNDS))
        def _():
            g_pass(layer - 2)

        @pl.when((layer >= 3) & (layer < 3 + ROUNDS))
        def _():
            e_pass(layer - 3)

    for piece in range(4):
        for step in others:
            own_row(piece, step).start()

    def settle(v):
        @pl.loop(0, ROUNDS)
        def _(u):
            for piece in range(4):
                g_own(u, piece, v + 1).wait()
                for step in range(4):
                    f_copy(u, piece, step, v + 1).wait()

    when_is(x, range(4), settle)

    def settle_h(n):
        @pl.loop(0, ROUNDS)
        def _(u):
            for piece in (0, 2):
                for step in range(4):
                    h_copy(u, piece, step, n).wait()

    when_is(taken, range(1, 5), settle_h)

    fetch(0)
    mine = x * 2 + zh

    @pl.loop(0, KVH)
    def _(k):
        fetched(k)

        @pl.when(k + 1 < KVH)
        def _():
            fetch(k + 1)

        @pl.when(k == 0)
        def _():
            x_send(LAYERS - 1)

        @pl.when(k >= 2)
        def _():
            for g in range(GROUP):
                o_copy(k - 2, g).wait()

        slot = lax.rem(k, 2)
        obuf[slot] = head_group(mine, core, qbuf.at[slot], kbuf.at[slot], vbuf.at[slot], bias, s_ref, m_ref, l_ref, acc_ref)
        for g in range(GROUP):
            o_copy(k, g).start()

    for k in (KVH - 2, KVH - 1):
        for g in range(GROUP):
            o_copy(k, g).wait()
    for piece in range(4):
        for step in range(4):
            own_row(piece, step).wait()

    @pl.loop(0, ROUNDS)
    def _(u):
        for step in others:
            y0_copy(u, step).wait_send()

            def sent(v):
                for piece in range(4):
                    g_copy(u, piece, step, v + 1).wait_send()

            when_is(lax.rem(x + step, 4), range(4), sent)

        def z_sent(v):
            for step, flip in zorder:
                if step * 2 + flip:
                    z0_copy(u, step, flip, v == 1).wait_send()

        when_is(core, (0, 1), z_sent)

        def swapped(n):
            for piece in (0, 2):
                for step in range(4):
                    e_copy(u, piece, step, n).wait_send()

        when_is(given, range(1, 5), swapped)

    @pl.loop(1, LAYERS)
    def _(layer):
        for step in others:
            y_copy(layer, step).wait_send()
        for step, flip in zorder:
            if step * 2 + flip:
                z_copy(layer, step, flip).wait_send()
        for piece in range(4):
            for step in range(4):
                x_copy(layer, step, piece).wait()


def relay(cache, queries, bias):
    dma = pltpu.SemaphoreType.DMA
    bf = jnp.bfloat16
    f32 = jnp.float32
    rows = GROUP * 256
    anyspace = pl.BlockSpec(memory_space=pl.ANY)
    sems = [
        (4, 3), (4, 3), (4,), (7, 3), (7, 3), (7,), (4, 8), (4, 8), (7, 8), (7, 8), (4, 4, 3), (4, 4, 3), (4, 4),
        (4, 4, 4), (4, 4, 4), (4, 2, 4), (4, 2, 4), (4, 2, 4), (4, 2, 4), (7, 3, 4), (7, 3, 4), (7, 4), (4, 4),
        (2,), (2,), (2, 4), (2, 4),
    ]
    return pl.pallas_call(
        relay_kernel,
        out_shape=(
            jax.ShapeDtypeStruct((LAYERS, 256, 2048), bf),
            jax.ShapeDtypeStruct((256, QH * HD), bf),
            jax.ShapeDtypeStruct((CHUNKS, 4, 2, SEQD, HD), bf),
            jax.ShapeDtypeStruct((LAYERS, 2, 2, 2, 2, 256, HD), bf),
        ),
        in_specs=[anyspace, anyspace, pl.BlockSpec(memory_space=pltpu.VMEM)],
        out_specs=(anyspace,) * 4,
        scratch_shapes=[
            pltpu.VMEM((4, 4, 2, 256, HD), bf),
            pltpu.VMEM((LAYERS - 1, 4, 4, 256, HD), bf),
            pltpu.VMEM((2, 4, 2, SEQD, HD), bf),
            pltpu.VMEM((2, 4, 2, SEQD, HD), bf),
            pltpu.VMEM((2, rows, HD), bf),
            pltpu.VMEM((2, rows, HD), bf),
            pltpu.VMEM((8, rows, SEQD), f32),
            pltpu.VMEM((rows, 128), f32),
            pltpu.VMEM((rows, 128), f32),
            pltpu.VMEM((rows, HD), f32),
        ]
        + [dma(shape) for shape in sems],
        compiler_params=pltpu.CompilerParams(has_side_effects=True, vmem_limit_bytes=56 << 20),
    )(cache.reshape(LAYERS, 2, 2, 2, 2, 256, HD), queries, bias)


def key_bias(section_counts, summary_blocks):
    chosen = (jnp.arange(8) == lax.axis_index("doc")).astype(jnp.int32)
    counts = jnp.sum(section_counts.reshape(8, 8) * chosen[None, :], axis=1)
    blocks = jnp.sum(summary_blocks.reshape(8, 8, SECTIONS) * chosen[None, :, None], axis=1)
    live_section = jnp.arange(SECTIONS)[None, :] < counts[:, None]
    live_slot = jnp.arange(SUMLEN)[None, None, :] < BLOCK * blocks[:, :, None]
    live = (live_section[:, :, None] & live_slot).reshape(8, SEQD)
    return jnp.where(live, 0.0, NEGATIVE).astype(jnp.float32)


def local(summary_cache, queries, section_counts, summary_blocks):
    bias = key_bias(section_counts, summary_blocks)
    relayed, attended, _, _ = relay(summary_cache, queries[0], bias)
    return attended[None], relayed[:, None]


def solution(mesh):
    placed = (P(None, "doc", None, "ctx"), P("doc", "ctx", None), P(), P())
    return jax.shard_map(
        local,
        mesh=mesh,
        in_specs=placed,
        out_specs=(P("doc", "ctx", None), P(None, "doc", "ctx", None)),
        check_vma=False,
    )
```

time: 563 us -> 245 us (0.44)
  the two profiles are of different devices: /device:TPU:30 before, /device:TPU:103 now
where the time goes in v2:
time: 245 us
  Pallas kernels  230 us (94%)
  local copies, waits for them, and re-layouts  13.2 us (5%)
    pallas_call x1, Pallas kernels, relay(): pl.pallas_call(relay_kernel, out_shape=(jax.ShapeDtypeStruct((LAYERS, 256...  230 us
    unnamed x4, local copies, waits for them, and re-layouts  11.6 us

profile of v2, /device:TPU:103, one launch (start us, length us, event | category | flops | bytes accessed | tf_op | source)
XLA Modules:
  0.0 244.5 jit_solution(1547070011231189614)
XLA Ops:
  0.7 0.7 reshape.53
  1.4 0.1 multiply_reduce_fusion.1
  1.5 0.1 and.12
  1.6 0.8 reshape.54
  2.4 0.1 multiply_reduce_fusion
  2.5 0.1 lt.43
  2.6 0.6 and_select_fusion.bias
  3.2 229.7 %shard_map.59 = (bf16[8,256,2048]{2,1,0:T(8,128)(2,1)}, bf16[256,4096]{1,0:T(8,128)(2,1)}, bf16[16,4,2,512,128]{4,3,2,1,0:T(8,128)(2,1)}, bf16[8,2,2,2,2,256,128]{6,5,4,3,2,1,0:T(8,128)(2,1)}) custom-call(bf16[8,2,2,2,2,256,128]{6,5,4,3,2,1,0:T(8,128)(2,1)} %bitcast.13, bf16[256,4096]{1,0:T(8,128)(2,1)} %bitcast.15, f32[8,512]{1,0:T(8,128)} %and_select_fusion.bias), custom_call_target="tpu_custom_call" | custom-call | tf_op jit(solution)/shard_map/pallas_call | solution.py:465
  233.0 3.1 %copy.10 = bf16[1,256,4096]{2,1,0:T(8,128)(2,1)} copy(bf16[1,256,4096]{2,1,0:T(8,128)(2,1)} %bitcast.16) | data formatting | bytes 4194304
  236.1 8.4 %copy.11 = bf16[8,1,256,2048]{3,2,1,0:T(8,128)(2,1)} copy(bf16[8,1,256,2048]{3,2,1,0:T(8,128)(2,1)} %bitcast.14) | data formatting | bytes 16777216
  (5 shorter events, 0.0 us)

commit v3 on v2

v3 whole, which is shorter than its diff:
```python
import functools
import math

import jax
import jax.numpy as jnp
from jax import lax
from jax.experimental import pallas as pl
from jax.experimental.pallas import tpu as pltpu
from jax.sharding import PartitionSpec as P

QH = 32
KVH = 8
HD = 128
BLOCK = 128
SECTIONS = 2
GROUP = 4
SUMLEN = 256
SEQD = 512
LAYERS = 8
GSEQ = 4096
CHUNKS = 16
NEGATIVE = -1e30
MESH = pl.DeviceIdType.MESH
SCALE = (1.0 / math.sqrt(HD)) * math.log2(math.e)


def place(x, y, z, core):
    return (lax.rem(z, 2) * 4 + y, x * 4 + (z // 2) * 2 + core)


def head_group(mine, half, q_ref, k_ref, v_ref, bias_ref, s_ref, m_ref, l_ref, acc_ref):
    rows = q_ref.shape[0]

    def score(doc, diagonal):
        k = k_ref[doc // 2, lax.rem(doc, 2)]
        s = lax.dot_general(q_ref[...], k, (((1,), (1,)), ((), ())), preferred_element_type=jnp.float32)
        s = s * SCALE + bias_ref[pl.ds(doc, 1), :]
        if diagonal:
            at = lax.rem(lax.broadcasted_iota(jnp.int32, s.shape, 0), 256) + half * 256
            s = jnp.where(lax.broadcasted_iota(jnp.int32, s.shape, 1) <= at, s, NEGATIVE)
        s_ref[doc] = s
        top = jnp.maximum(jnp.maximum(s[:, 0:128], s[:, 128:256]), jnp.maximum(s[:, 256:384], s[:, 384:512]))
        return top

    def weigh(doc):
        v = v_ref[doc // 2, lax.rem(doc, 2)]
        top = m_ref[...]
        w = [jnp.exp2(s_ref[doc, :, i * 128 : (i + 1) * 128] - top) for i in range(4)]
        part = (w[0] + w[1]) + (w[2] + w[3])
        pair = [jnp.concatenate([w[2 * i].astype(jnp.bfloat16), w[2 * i + 1].astype(jnp.bfloat16)], axis=1) for i in range(2)]
        summed = lax.dot_general(
            jnp.concatenate(pair, axis=1), v, (((1,), (0,)), ((), ())), preferred_element_type=jnp.float32
        )
        return part, summed

    m_ref[...] = score(mine, True)

    @pl.loop(0, mine)
    def _(doc):
        m_ref[...] = jnp.maximum(m_ref[...], score(doc, False))

    m_ref[...] = jnp.broadcast_to(jnp.max(m_ref[...], axis=1, keepdims=True), m_ref.shape)
    part, summed = weigh(mine)
    l_ref[...] = part
    acc_ref[...] = summed

    @pl.loop(0, mine)
    def _(doc):
        part, summed = weigh(doc)
        l_ref[...] += part
        acc_ref[...] += summed

    return (acc_ref[...] / jnp.sum(l_ref[...], axis=1, keepdims=True)).astype(jnp.bfloat16)


ROUNDS = 4
PART = SEQD // ROUNDS


def relay_kernel(
    cache, queries, bias, out, attended, ybuf, keys, zbuf, qbuf, obuf, s_ref, m_ref, l_ref, acc_ref,
    y0s, y0r, y0o, ys, yr, yo, z0s, z0r, z0o, zs, zr, gs, gr, xs, xr, xo, ls, lr, qs, qr, os, rs,
):
    d = lax.axis_index("doc")
    c = lax.axis_index("ctx")
    zl, y = d // 4, lax.rem(d, 4)
    x, zh, core = c // 4, lax.rem(c // 2, 2), lax.rem(c, 2)
    z = zh * 2 + zl
    chunk = zh * 2 + core
    others = (1, 3, 2)

    def remote(src, dst, ssem, rsem, dev):
        return pltpu.make_async_remote_copy(src, dst, ssem, rsem, device_id=dev, device_id_type=MESH)

    def when_is(value, options, body):
        for v in options:
            @pl.when(value == v)
            def _():
                body(v)

    def part(u):
        return pl.ds(pl.multiple_of(u * PART, PART), PART)

    def half_rows(half):
        return pl.ds(pl.multiple_of(half * 256, 256), 256)

    def head_cols(h):
        return pl.ds(pl.multiple_of(h * HD, HD), HD)

    def y_copy(layer, step, u=None):
        to = lax.rem(y + step, 4)
        src = cache.at[layer, :, to // 2, lax.rem(to, 2)]
        dst = ybuf.at[layer, y // 2, lax.rem(y, 2)]
        if u is None:
            ssem, rsem, own, at = ys, yr, yo, layer - 1
        else:
            ssem, rsem, own, at = y0s, y0r, y0o, u
            src, dst = src.at[:, part(u)], dst.at[:, part(u)]
        if step == 0:
            return pltpu.make_async_copy(src, dst, own.at[at])
        return remote(src, dst, ssem.at[at, step - 1], rsem.at[at, step - 1], place(x, to, z, core))

    def y_wait(layer, u=None):
        for step in others:
            y_copy(layer, step, u).wait_recv()
        y_copy(layer, 0, u).wait()

    def z0_copy(u, flip):
        to = lax.rem(zl + flip, 2)
        src = ybuf.at[0, :, :, to, part(u)]
        dst = keys.at[x, pl.ds(zl * 2, 2), :, part(u)]
        if flip == 0:
            return pltpu.make_async_copy(src, dst, z0o.at[u])
        return remote(src, dst, z0s.at[u], z0r.at[u], place(x, y, zh * 2 + to, core))

    def g_copy(u, step, n):
        to = lax.rem(x + step, 4)
        ref = keys.at[x, pl.ds(0, n), :, part(u)]
        return remote(ref, ref, gs.at[u, step - 1], gr.at[u, step - 1], place(to, y, z, core))

    def peer(rel):
        return lax.rem(zh + rel // 2, 2), lax.rem(core + lax.rem(rel, 2), 2)

    def peer_place(rel):
        to_zh, to_core = peer(rel)
        return place(x, y, to_zh * 2 + zl, to_core)

    def l_copy(frm, rel):
        to_zh, to_core = peer(rel)
        src = keys.at[frm, x, to_zh, half_rows(to_core)]
        dst = out.at[0, :, head_cols(frm * 4 + chunk)]
        if rel == 0:
            return pltpu.make_async_copy(src, dst, lr.at[frm, 0])
        return remote(src, dst, ls.at[frm, rel], lr.at[frm, rel], peer_place(rel))

    def q_copy(kv, g, rel):
        to_zh, to_core = peer(rel)
        src = queries.at[:, head_cols((kv * 4 + to_zh * 2 + to_core) * GROUP + g)]
        dst = qbuf.at[kv, chunk, pl.ds(g * 256, 256)]
        if rel == 0:
            return pltpu.make_async_copy(src, dst, qr.at[kv, g, 0])
        return remote(src, dst, qs.at[kv, g, rel], qr.at[kv, g, rel], peer_place(rel))

    def o_copy(kv, g, rel, away):
        to_zh, to_core = peer(rel)
        src = obuf.at[kv, to_zh * 2 + to_core, pl.ds(g * 256, 256)]
        dst = attended.at[:, head_cols((kv * 4 + chunk) * GROUP + g)]
        if not away:
            return pltpu.make_async_copy(src, dst, rs.at[kv, g, 0])
        return remote(src, dst, os.at[kv, g, rel], rs.at[kv, g, rel], peer_place(rel))

    zorder = ((1, 0), (1, 1), (3, 0), (3, 1), (2, 0), (2, 1), (0, 1), (0, 0))

    def z_copy(layer, step, flip):
        to_z, to_core = lax.rem(z + step, 4), lax.rem(core + flip, 2)
        r = step * 2 + flip
        src = ybuf.at[layer, :, to_z // 2, lax.rem(to_z, 2), half_rows(to_core)]
        dst = zbuf.at[layer - 1, pl.ds(zl * 2, 2), chunk]
        if r == 0:
            return pltpu.make_async_copy(src, dst, zr.at[layer - 1, 0])
        return remote(src, dst, zs.at[layer - 1, r], zr.at[layer - 1, r], place(x, y, to_z, to_core))

    def x_copy(layer, step, piece):
        to = lax.rem(x + step, 4)
        src = zbuf.at[layer - 1, to, piece]
        dst = out.at[layer, :, head_cols(x * 4 + piece)]
        if step == 0:
            return pltpu.make_async_copy(src, dst, xo.at[layer - 1, piece])
        return remote(src, dst, xs.at[layer - 1, step - 1, piece], xr.at[layer - 1, step - 1, piece], place(to, y, z, core))

    def z_send(layer):
        y_wait(layer)
        for step, flip in zorder:
            z_copy(layer, step, flip).start()

    def x_send(layer):
        for step, flip in zorder:
            if step * 2 + flip == 0:
                z_copy(layer, 0, 0).wait()
            else:
                z_copy(layer, step, flip).wait_recv()
        for step in (1, 3, 2, 0):
            for piece in range(4):
                x_copy(layer, step, piece).start()

    @pl.loop(0, ROUNDS)
    def _(u):
        for step in others + (0,):
            y_copy(0, step, u).start()

    @pl.loop(1, LAYERS)
    def _(layer):
        for step in others + (0,):
            y_copy(layer, step).start()

    @pl.loop(0, ROUNDS + 1)
    def _(t):
        @pl.when(t < ROUNDS)
        def _():
            y_wait(0, t)
            z0_copy(t, 1).start()
            z0_copy(t, 0).start()

        @pl.when(t >= 1)
        def _():
            z0_copy(t - 1, 1).wait_recv()
            z0_copy(t - 1, 0).wait()
            for step in others:
                when_is(lax.rem(x + step, 4), range(4), lambda v: g_copy(t - 1, step, v + 1).start())

    for rel in (3, 2, 1, 0):
        for kv in range(2):
            for g in range(GROUP):
                q_copy(kv, g, rel).start()

    @pl.loop(1, 4)
    def _(layer):
        z_send(layer)

    def gathered(v):
        @pl.loop(0, ROUNDS)
        def _(u):
            for step in others:
                g_copy(u, step, v + 1).wait_recv()

    when_is(x, range(4), gathered)
    x_send(1)

    @pl.loop(0, 8)
    def _(t):
        rel = 3 - t // 2
        kv = lax.rem(t, 2)
        to_zh, to_core = peer(rel)
        for g in range(GROUP):
            pltpu.make_async_copy(queries.at[:, head_cols(g)], qbuf.at[kv, 0, pl.ds(g * 256, 256)], qr.at[kv, g, rel]).wait()
        src = to_zh * 2 + to_core
        obuf[kv, src] = head_group(
            x * 2 + to_zh, to_core, qbuf.at[kv, src], keys.at[kv], keys.at[2 + kv], bias, s_ref, m_ref, l_ref, acc_ref
        )

        @pl.when(t < 4)
        def _():
            z_send(t + 4)

        @pl.when(t < 6)
        def _():
            x_send(t + 2)
            for g in range(GROUP):
                o_copy(kv, g, rel, True).start()

        @pl.when(t >= 6)
        def _():
            for g in range(GROUP):
                o_copy(kv, g, 0, False).start()

        @pl.when(t == 4)
        def _():
            for rel in (3, 2, 1, 0):
                for frm in range(4):
                    l_copy(frm, rel).start()

    @pl.loop(0, ROUNDS)
    def _(u):
        for step in others:
            y_copy(0, step, u).wait_send()
            when_is(lax.rem(x + step, 4), range(4), lambda v: g_copy(u, step, v + 1).wait_send())
        z0_copy(u, 1).wait_send()

    for kv in range(2):
        for g in range(GROUP):
            o_copy(kv, g, 0, False).wait()
            for rel in (1, 2, 3):
                q_copy(kv, g, rel).wait_send()
                o_copy(kv, g, rel, True).wait()

    for frm in range(4):
        for rel in range(4):
            l_copy(frm, rel).wait()

    @pl.loop(1, LAYERS)
    def _(layer):
        for step in others:
            y_copy(layer, step).wait_send()
        for step, flip in zorder:
            if step * 2 + flip:
                z_copy(layer, step, flip).wait_send()
        for piece in range(4):
            for step in range(4):
                x_copy(layer, step, piece).wait()


def relay(cache, queries, bias):
    dma = pltpu.SemaphoreType.DMA
    bf = jnp.bfloat16
    f32 = jnp.float32
    rows = GROUP * 256
    anyspace = pl.BlockSpec(memory_space=pl.ANY)
    sems = [
        (4, 3), (4, 3), (4,), (7, 3), (7, 3), (7,), (4,), (4,), (4,), (7, 8), (7, 8), (4, 3), (4, 3),
        (7, 3, 4), (7, 3, 4), (7, 4), (4, 4), (4, 4), (2, 4, 4), (2, 4, 4), (2, 4, 4), (2, 4, 4),
    ]
    return pl.pallas_call(
        relay_kernel,
        out_shape=(
            jax.ShapeDtypeStruct((LAYERS, 256, 2048), bf),
            jax.ShapeDtypeStruct((256, QH * HD), bf),
            jax.ShapeDtypeStruct((LAYERS, 2, 2, 2, SEQD, HD), bf),
        ),
        in_specs=[anyspace, anyspace, pl.BlockSpec(memory_space=pltpu.VMEM)],
        out_specs=(anyspace,) * 3,
        scratch_shapes=[
            pltpu.VMEM((4, 4, 2, SEQD, HD), bf),
            pltpu.VMEM((LAYERS - 1, 4, 4, 256, HD), bf),
            pltpu.VMEM((2, 4, rows, HD), bf),
            pltpu.VMEM((2, 4, rows, HD), bf),
            pltpu.VMEM((8, rows, SEQD), f32),
            pltpu.VMEM((rows, 128), f32),
            pltpu.VMEM((rows, 128), f32),
            pltpu.VMEM((rows, HD), f32),
        ]
        + [dma(shape) for shape in sems],
        compiler_params=pltpu.CompilerParams(has_side_effects=True, vmem_limit_bytes=56 << 20),
    )(cache.reshape(LAYERS, 2, 2, 2, SEQD, HD), queries, bias)


def key_bias(section_counts, summary_blocks):
    chosen = (jnp.arange(8) == lax.axis_index("doc")).astype(jnp.int32)
    counts = jnp.sum(section_counts.reshape(8, 8) * chosen[None, :], axis=1)
    blocks = jnp.sum(summary_blocks.reshape(8, 8, SECTIONS) * chosen[None, :, None], axis=1)
    live_section = jnp.arange(SECTIONS)[None, :] < counts[:, None]
    live_slot = jnp.arange(SUMLEN)[None, None, :] < BLOCK * blocks[:, :, None]
    live = (live_section[:, :, None] & live_slot).reshape(8, SEQD)
    return jnp.where(live, 0.0, NEGATIVE).astype(jnp.float32)


def local(summary_cache, queries, section_counts, summary_blocks):
    bias = key_bias(section_counts, summary_blocks)
    relayed, attended, _ = relay(summary_cache, queries[0], bias)
    return attended[None], relayed[:, None]


def solution(mesh):
    placed = (P(None, "doc", None, "ctx"), P("doc", "ctx", None), P(), P())
    return jax.shard_map(
        local,
        mesh=mesh,
        in_specs=placed,
        out_specs=(P("doc", "ctx", None), P(None, "doc", "ctx", None)),
        check_vma=False,
    )
```

time: 245 us -> 190 us (0.78)
  the two profiles are of different devices: /device:TPU:103 before, /device:TPU:30 now
where the time goes in v3:
time: 190 us; the launch traced here: 188 us
  Pallas kernels  173 us (91%)
  local copies, waits for them, and re-layouts  13.2 us (7%)
    pallas_call x1, Pallas kernels, relay(): pl.pallas_call(relay_kernel, out_shape=(jax.ShapeDtypeStruct((LAYERS, 256...  173 us
    unnamed x4, local copies, waits for them, and re-layouts  11.6 us

profile of v3, /device:TPU:30, one launch (start us, length us, event | category | flops | bytes accessed | tf_op | source)
XLA Modules:
  0.0 188.1 jit_solution(880797724902062002)
XLA Ops:
  0.7 0.7 reshape.53
  1.4 0.1 multiply_reduce_fusion.1
  1.5 0.1 and.12
  1.6 0.8 reshape.54
  2.4 0.1 multiply_reduce_fusion
  2.5 0.1 lt.43
  2.6 0.6 and_select_fusion.bias
  3.2 173.3 %shard_map.59 = (bf16[8,256,2048]{2,1,0:T(8,128)(2,1)}, bf16[256,4096]{1,0:T(8,128)(2,1)}, bf16[8,2,2,2,512,128]{5,4,3,2,1,0:T(8,128)(2,1)}) custom-call(bf16[8,2,2,2,512,128]{5,4,3,2,1,0:T(8,128)(2,1)} %bitcast.13, bf16[256,4096]{1,0:T(8,128)(2,1)} %bitcast.15, f32[8,512]{1,0:T(8,128)} %and_select_fusion.bias), custom_call_target="tpu_custom_call" | custom-call | tf_op jit(solution)/shard_map/pallas_call | solution.py:322
  176.6 3.1 %copy.10 = bf16[1,256,4096]{2,1,0:T(8,128)(2,1)} copy(bf16[1,256,4096]{2,1,0:T(8,128)(2,1)} %bitcast.16) | data formatting | bytes 4194304
  179.7 8.4 %copy.11 = bf16[8,1,256,2048]{3,2,1,0:T(8,128)(2,1)} copy(bf16[8,1,256,2048]{3,2,1,0:T(8,128)(2,1)} %bitcast.14) | data formatting | bytes 16777216
  (5 shorter events, 0.0 us)

commit v4 on v3

--- a/solution.py
+++ b/solution.py
@@ -79,7 +79,7 @@
 
 def relay_kernel(
     cache, queries, bias, out, attended, ybuf, keys, zbuf, qbuf, obuf, s_ref, m_ref, l_ref, acc_ref,
-    y0s, y0r, y0o, ys, yr, yo, z0s, z0r, z0o, zs, zr, gs, gr, xs, xr, xo, ls, lr, qs, qr, os, rs,
+    y0s, y0r, y0o, ys, yr, yo, z0s, z0r, z0o, zs, zr, gs, gr, xs, xr, ls, lr, qs, qr, os, rs,
 ):
     d = lax.axis_index("doc")
     c = lax.axis_index("ctx")
@@ -149,8 +149,6 @@
         to_zh, to_core = peer(rel)
         src = keys.at[frm, x, to_zh, half_rows(to_core)]
         dst = out.at[0, :, head_cols(frm * 4 + chunk)]
-        if rel == 0:
-            return pltpu.make_async_copy(src, dst, lr.at[frm, 0])
         return remote(src, dst, ls.at[frm, rel], lr.at[frm, rel], peer_place(rel))
 
     def q_copy(kv, g, rel):
@@ -161,12 +159,10 @@
             return pltpu.make_async_copy(src, dst, qr.at[kv, g, 0])
         return remote(src, dst, qs.at[kv, g, rel], qr.at[kv, g, rel], peer_place(rel))
 
-    def o_copy(kv, g, rel, away):
+    def o_copy(kv, g, rel):
         to_zh, to_core = peer(rel)
         src = obuf.at[kv, to_zh * 2 + to_core, pl.ds(g * 256, 256)]
         dst = attended.at[:, head_cols((kv * 4 + chunk) * GROUP + g)]
-        if not away:
-            return pltpu.make_async_copy(src, dst, rs.at[kv, g, 0])
         return remote(src, dst, os.at[kv, g, rel], rs.at[kv, g, rel], peer_place(rel))
 
     zorder = ((1, 0), (1, 1), (3, 0), (3, 1), (2, 0), (2, 1), (0, 1), (0, 0))
@@ -184,8 +180,6 @@
         to = lax.rem(x + step, 4)
         src = zbuf.at[layer - 1, to, piece]
         dst = out.at[layer, :, head_cols(x * 4 + piece)]
-        if step == 0:
-            return pltpu.make_async_copy(src, dst, xo.at[layer - 1, piece])
         return remote(src, dst, xs.at[layer - 1, step - 1, piece], xr.at[layer - 1, step - 1, piece], place(to, y, z, core))
 
     def z_send(layer):
@@ -199,9 +193,11 @@
                 z_copy(layer, 0, 0).wait()
             else:
                 z_copy(layer, step, flip).wait_recv()
-        for step in (1, 3, 2, 0):
+        for step in others:
             for piece in range(4):
                 x_copy(layer, step, piece).start()
+        for piece in range(4):
+            out[layer, :, head_cols(x * 4 + piece)] = zbuf[layer - 1, x, piece]
 
     @pl.loop(0, ROUNDS)
     def _(u):
@@ -213,6 +209,13 @@
         for step in others + (0,):
             y_copy(layer, step).start()
 
+    def q_send(kv, g):
+        for rel in (3, 2, 1, 0):
+            q_copy(kv, g, rel).start()
+
+    for g in range(2):
+        q_send(0, g)
+
     @pl.loop(0, ROUNDS + 1)
     def _(t):
         @pl.when(t < ROUNDS)
@@ -228,10 +231,11 @@
             for step in others:
                 when_is(lax.rem(x + step, 4), range(4), lambda v: g_copy(t - 1, step, v + 1).start())
 
-    for rel in (3, 2, 1, 0):
-        for kv in range(2):
-            for g in range(GROUP):
-                q_copy(kv, g, rel).start()
+        when_is(t, range(2), lambda v: q_send(0, 2 + v))
+        when_is(t, range(2, 4), lambda v: q_send(1, v - 2))
+
+    for g in range(2, GROUP):
+        q_send(1, g)
 
     @pl.loop(1, 4)
     def _(layer):
@@ -262,22 +266,38 @@
         def _():
             z_send(t + 4)
 
-        @pl.when(t < 6)
-        def _():
-            x_send(t + 2)
+        @pl.when((t < 6) & (t != 2))
+        def _():
+            x_send(t + 2 - t // 3)
+
+        @pl.when(t == 3)
+        def _():
+            for rel in (3, 2):
+                for kv in range(2):
+                    for g in range(GROUP):
+                        o_copy(kv, g, rel).start()
+
+        @pl.when((t == 4) | (t == 5))
+        def _():
             for g in range(GROUP):
-                o_copy(kv, g, rel, True).start()
+                o_copy(kv, g, 1).start()
 
         @pl.when(t >= 6)
         def _():
             for g in range(GROUP):
-                o_copy(kv, g, 0, False).start()
+                attended[:, head_cols((kv * 4 + chunk) * GROUP + g)] = obuf[kv, chunk, pl.ds(g * 256, 256)]
 
         @pl.when(t == 4)
         def _():
-            for rel in (3, 2, 1, 0):
+            for rel in (3, 2, 1):
                 for frm in range(4):
                     l_copy(frm, rel).start()
+            for frm in range(4):
+                out[0, :, head_cols(frm * 4 + chunk)] = keys[frm, x, zh, half_rows(core)]
+
+        @pl.when(t == 7)
+        def _():
+            x_send(7)
 
     @pl.loop(0, ROUNDS)
     def _(u):
@@ -288,13 +308,12 @@
 
     for kv in range(2):
         for g in range(GROUP):
-            o_copy(kv, g, 0, False).wait()
             for rel in (1, 2, 3):
                 q_copy(kv, g, rel).wait_send()
-                o_copy(kv, g, rel, True).wait()
+                o_copy(kv, g, rel).wait()
 
     for frm in range(4):
-        for rel in range(4):
+        for rel in (1, 2, 3):
             l_copy(frm, rel).wait()
 
     @pl.loop(1, LAYERS)
@@ -305,7 +324,7 @@
             if step * 2 + flip:
                 z_copy(layer, step, flip).wait_send()
         for piece in range(4):
-            for step in range(4):
+            for step in others:
                 x_copy(layer, step, piece).wait()
 
 
@@ -317,7 +336,7 @@
     anyspace = pl.BlockSpec(memory_space=pl.ANY)
     sems = [
         (4, 3), (4, 3), (4,), (7, 3), (7, 3), (7,), (4,), (4,), (4,), (7, 8), (7, 8), (4, 3), (4, 3),
-        (7, 3, 4), (7, 3, 4), (7, 4), (4, 4), (4, 4), (2, 4, 4), (2, 4, 4), (2, 4, 4), (2, 4, 4),
+        (7, 3, 4), (7, 3, 4), (4, 4), (4, 4), (2, 4, 4), (2, 4, 4), (2, 4, 4), (2, 4, 4),
     ]
     return pl.pallas_call(
         relay_kernel,
@@ -326,8 +345,8 @@
             jax.ShapeDtypeStruct((256, QH * HD), bf),
             jax.ShapeDtypeStruct((LAYERS, 2, 2, 2, SEQD, HD), bf),
         ),
-        in_specs=[anyspace, anyspace, pl.BlockSpec(memory_space=pltpu.VMEM)],
-        out_specs=(anyspace,) * 3,
+        in_specs=[pl.BlockSpec(memory_space=pltpu.HBM)] * 2 + [pl.BlockSpec(memory_space=pltpu.VMEM)],
+        out_specs=(pl.BlockSpec(memory_space=pltpu.VMEM),) * 2 + (anyspace,),
         scratch_shapes=[
             pltpu.VMEM((4, 4, 2, SEQD, HD), bf),
             pltpu.VMEM((LAYERS - 1, 4, 4, 256, HD), bf),
@@ -339,8 +358,29 @@
             pltpu.VMEM((rows, HD), f32),
         ]
         + [dma(shape) for shape in sems],
-        compiler_params=pltpu.CompilerParams(has_side_effects=True, vmem_limit_bytes=56 << 20),
+        compiler_params=pltpu.CompilerParams(has_side_effects=True, vmem_limit_bytes=40 << 20),
     )(cache.reshape(LAYERS, 2, 2, 2, SEQD, HD), queries, bias)
+
+
+def settle_kernel(out, attended, out_to, attended_to, sems):
+    copies = [pltpu.make_async_copy(out.at[layer], out_to.at[layer], sems.at[layer]) for layer in range(LAYERS)]
+    copies.append(pltpu.make_async_copy(attended, attended_to, sems.at[LAYERS]))
+    for copy in copies:
+        copy.start()
+    for copy in copies:
+        copy.wait()
+
+
+def settle(out, attended):
+    vmem, anyspace = pl.BlockSpec(memory_space=pltpu.VMEM), pl.BlockSpec(memory_space=pl.ANY)
+    return pl.pallas_call(
+        settle_kernel,
+        out_shape=tuple(jax.ShapeDtypeStruct(a.shape, a.dtype) for a in (out, attended)),
+        in_specs=[vmem, vmem],
+        out_specs=(anyspace, anyspace),
+        scratch_shapes=[pltpu.SemaphoreType.DMA((LAYERS + 1,))],
+        compiler_params=pltpu.CompilerParams(vmem_limit_bytes=16 << 20),
+    )(out, attended)
 
 
 def key_bias(section_counts, summary_blocks):
@@ -356,6 +396,7 @@
 def local(summary_cache, queries, section_counts, summary_blocks):
     bias = key_bias(section_counts, summary_blocks)
     relayed, attended, _ = relay(summary_cache, queries[0], bias)
+    relayed, attended = settle(relayed, attended)
     return attended[None], relayed[:, None]
 
 

time: 190 us -> 175 us (0.921)
  local copies, waits for them, and re-layouts: 13.2 us -> 3.24 us
  Pallas kernels: 173 us -> 170 us
    unnamed x4, local copies, waits for them, and re-layouts: 11.6 us -> 1.6 us
    pallas_call x1, Pallas kernels: 173 us -> 166 us  [relay(): pl.pallas_call(relay_kernel, out_shape=(jax.ShapeDtypeStruct((LAYERS, 256...]
    pallas_call x0 -> x1, Pallas kernels: none -> 4.04 us  [settle(): pl.pallas_call(settle_kernel, out_shape=tuple((jax.ShapeDtypeStruct(a.sha...]
where the time goes in v4:
time: 175 us; the launch traced here: 174 us
  Pallas kernels  170 us (97%)
  local copies, waits for them, and re-layouts  3.24 us (2%)
    pallas_call x1, Pallas kernels, relay(): pl.pallas_call(relay_kernel, out_shape=(jax.ShapeDtypeStruct((LAYERS, 256...  166 us
    pallas_call x1, Pallas kernels, settle(): pl.pallas_call(settle_kernel, out_shape=tuple((jax.ShapeDtypeStruct(a.sha...  4.04 us

profile of v4, /device:TPU:30, one launch (start us, length us, event | category | flops | bytes accessed | tf_op | source)
XLA Modules:
  0.0 174.1 jit_solution(18005689626853207580)
XLA Ops:
  0.7 0.7 reshape.53
  1.4 0.1 multiply_reduce_fusion.1
  1.5 0.1 and.12
  1.6 0.8 reshape.54
  2.4 0.1 multiply_reduce_fusion
  2.5 0.1 lt.43
  2.6 0.0 copy-start
  2.6 1.6 copy-done
  4.2 165.8 %shard_map.59 = (bf16[8,256,2048]{2,1,0:T(8,128)(2,1)S(1)}, bf16[256,4096]{1,0:T(8,128)(2,1)S(1)}, bf16[8,2,2,2,512,128]{5,4,3,2,1,0:T(8,128)(2,1)}) custom-call(bf16[8,2,2,2,512,128]{5,4,3,2,1,0:T(8,128)(2,1)} %bitcast.14, bf16[256,4096]{1,0:T(8,128)(2,1)S(1)} %bitcast.13, f32[8,512]{1,0:T(8,128)S(1)} %and_select_fusion.bias), custom_call_target="tpu_custom_call" | custom-call | tf_op jit(solution)/shard_map/pallas_call | solution.py:341
  170.1 4.0 %shard_map.60 = (bf16[8,256,2048]{2,1,0:T(8,128)(2,1)}, bf16[256,4096]{1,0:T(8,128)(2,1)}) custom-call(bf16[8,256,2048]{2,1,0:T(8,128)(2,1)S(1)} %get-tuple-element.6.out, bf16[256,4096]{1,0:T(8,128)(2,1)S(1)} %get-tuple-element.7.attended), custom_call_target="tpu_custom_call" | custom-call | tf_op jit(solution)/shard_map/pallas_call | solution.py:376
  (6 shorter events, 0.0 us)
Async XLA Ops:
  2.6 1.6 copy-start

commit v5 on v4

--- a/solution.py
+++ b/solution.py
@@ -78,8 +78,8 @@
 
 
 def relay_kernel(
-    cache, queries, bias, out, attended, ybuf, keys, zbuf, qbuf, obuf, s_ref, m_ref, l_ref, acc_ref,
-    y0s, y0r, y0o, ys, yr, yo, z0s, z0r, z0o, zs, zr, gs, gr, xs, xr, ls, lr, qs, qr, os, rs,
+    cache, queries, counts_hbm, blocks_hbm, out, attended, ybuf, bias, counts, blocks, keys, zbuf, qbuf, obuf, s_ref, m_ref, l_ref, acc_ref,
+    y0s, y0r, y0o, ys, yr, yo, z0s, z0r, z0o, zs, zr, gs, gr, xs, xr, ls, lr, qs, qr, os, rs, cs,
 ):
     d = lax.axis_index("doc")
     c = lax.axis_index("ctx")
@@ -199,9 +199,22 @@
         for piece in range(4):
             out[layer, :, head_cols(x * 4 + piece)] = zbuf[layer - 1, x, piece]
 
+    barrier = pltpu.get_barrier_semaphore()
+    peers = [place(x, lax.rem(y + step, 4), z, core) for step in others]
+    peers += [place(lax.rem(x + step, 4), y, z, core) for step in others]
+    peers += [place(x, y, lax.rem(z + step, 4), lax.rem(core + flip, 2)) for step, flip in zorder if step or flip]
+    for peer_device in peers:
+        pl.semaphore_signal(barrier, inc=1, device_id=peer_device, device_id_type=MESH)
+    tables = [pltpu.make_async_copy(counts_hbm, counts, cs.at[0]), pltpu.make_async_copy(blocks_hbm, blocks, cs.at[1])]
+    for copy in tables:
+        copy.start()
+    for u in range(ROUNDS):
+        y_copy(0, 0, u).start()
+    pl.semaphore_wait(barrier, len(peers))
+
     @pl.loop(0, ROUNDS)
     def _(u):
-        for step in others + (0,):
+        for step in others:
             y_copy(0, step, u).start()
 
     @pl.loop(1, LAYERS)
@@ -236,6 +249,16 @@
 
     for g in range(2, GROUP):
         q_send(1, g)
+
+    for copy in tables:
+        copy.wait()
+    slot = lax.broadcasted_iota(jnp.int32, (1, SEQD), 1)
+    second = slot // SUMLEN
+    for doc in range(8):
+        at = doc * 8 + d
+        live_blocks = jnp.where(second == 0, blocks[at, 0], blocks[at, 1])
+        live = (second < counts[at]) & (slot - second * SUMLEN < BLOCK * live_blocks)
+        bias[doc : doc + 1, :] = jnp.where(live, 0.0, NEGATIVE)
 
     @pl.loop(1, 4)
     def _(layer):
@@ -328,7 +351,7 @@
                 x_copy(layer, step, piece).wait()
 
 
-def relay(cache, queries, bias):
+def relay(cache, queries, counts, blocks):
     dma = pltpu.SemaphoreType.DMA
     bf = jnp.bfloat16
     f32 = jnp.float32
@@ -336,7 +359,7 @@
     anyspace = pl.BlockSpec(memory_space=pl.ANY)
     sems = [
         (4, 3), (4, 3), (4,), (7, 3), (7, 3), (7,), (4,), (4,), (4,), (7, 8), (7, 8), (4, 3), (4, 3),
-        (7, 3, 4), (7, 3, 4), (4, 4), (4, 4), (2, 4, 4), (2, 4, 4), (2, 4, 4), (2, 4, 4),
+        (7, 3, 4), (7, 3, 4), (4, 4), (4, 4), (2, 4, 4), (2, 4, 4), (2, 4, 4), (2, 4, 4), (2,),
     ]
     return pl.pallas_call(
         relay_kernel,
@@ -345,9 +368,12 @@
             jax.ShapeDtypeStruct((256, QH * HD), bf),
             jax.ShapeDtypeStruct((LAYERS, 2, 2, 2, SEQD, HD), bf),
         ),
-        in_specs=[pl.BlockSpec(memory_space=pltpu.HBM)] * 2 + [pl.BlockSpec(memory_space=pltpu.VMEM)],
+        in_specs=[anyspace] * 4,
         out_specs=(pl.BlockSpec(memory_space=pltpu.VMEM),) * 2 + (anyspace,),
         scratch_shapes=[
+            pltpu.VMEM((8, SEQD), f32),
+            pltpu.SMEM((64,), jnp.int32),
+            pltpu.SMEM((64, SECTIONS), jnp.int32),
             pltpu.VMEM((4, 4, 2, SEQD, HD), bf),
             pltpu.VMEM((LAYERS - 1, 4, 4, 256, HD), bf),
             pltpu.VMEM((2, 4, rows, HD), bf),
@@ -358,8 +384,8 @@
             pltpu.VMEM((rows, HD), f32),
         ]
         + [dma(shape) for shape in sems],
-        compiler_params=pltpu.CompilerParams(has_side_effects=True, vmem_limit_bytes=40 << 20),
-    )(cache.reshape(LAYERS, 2, 2, 2, SEQD, HD), queries, bias)
+        compiler_params=pltpu.CompilerParams(collective_id=0, has_side_effects=True, vmem_limit_bytes=40 << 20),
+    )(cache.reshape(LAYERS, 2, 2, 2, SEQD, HD), queries, counts, blocks)
 
 
 def settle_kernel(out, attended, out_to, attended_to, sems):
@@ -383,19 +409,8 @@
     )(out, attended)
 
 
-def key_bias(section_counts, summary_blocks):
-    chosen = (jnp.arange(8) == lax.axis_index("doc")).astype(jnp.int32)
-    counts = jnp.sum(section_counts.reshape(8, 8) * chosen[None, :], axis=1)
-    blocks = jnp.sum(summary_blocks.reshape(8, 8, SECTIONS) * chosen[None, :, None], axis=1)
-    live_section = jnp.arange(SECTIONS)[None, :] < counts[:, None]
-    live_slot = jnp.arange(SUMLEN)[None, None, :] < BLOCK * blocks[:, :, None]
-    live = (live_section[:, :, None] & live_slot).reshape(8, SEQD)
-    return jnp.where(live, 0.0, NEGATIVE).astype(jnp.float32)
-
-
 def local(summary_cache, queries, section_counts, summary_blocks):
-    bias = key_bias(section_counts, summary_blocks)
-    relayed, attended, _ = relay(summary_cache, queries[0], bias)
+    relayed, attended, _ = relay(summary_cache, queries[0], section_counts, summary_blocks)
     relayed, attended = settle(relayed, attended)
     return attended[None], relayed[:, None]
 

time: 175 us -> 173 us (0.989)
  the two profiles are of different devices: /device:TPU:30 before, /device:TPU:51 now
where the time goes in v5:
time: 173 us
  Pallas kernels  169 us (98%)
  local copies, waits for them, and re-layouts  3.01 us (2%)
    pallas_call x1, Pallas kernels, relay(): pl.pallas_call(relay_kernel, out_shape=(jax.ShapeDtypeStruct((LAYERS, 256...  165 us
    pallas_call x1, Pallas kernels, settle(): pl.pallas_call(settle_kernel, out_shape=tuple((jax.ShapeDtypeStruct(a.sha...  4.04 us

profile of v5, /device:TPU:51, one launch (start us, length us, event | category | flops | bytes accessed | tf_op | source)
XLA Modules:
  0.0 172.6 jit_solution(6879598549309826650)
XLA Ops:
  0.6 0.8 copy.6.blocks_hbm
  1.4 0.0 copy-start
  1.4 1.6 copy-done
  3.0 0.0 copy-start.1
  3.0 0.7 copy-done.1
  3.6 164.9 %shard_map.59 = (bf16[8,256,2048]{2,1,0:T(8,128)(2,1)S(1)}, bf16[256,4096]{1,0:T(8,128)(2,1)S(1)}, bf16[8,2,2,2,512,128]{5,4,3,2,1,0:T(8,128)(2,1)}) custom-call(bf16[8,2,2,2,512,128]{5,4,3,2,1,0:T(8,128)(2,1)} %bitcast.7, bf16[256,4096]{1,0:T(8,128)(2,1)S(1)} %bitcast.6, s32[64]{0:T(128)S(1)} %copy-done.1, s32[64,2]{1,0:T(8,128)S(1)} %copy.6.blocks_hbm), custom_call_target="tpu_custom_call" | custom-call | tf_op jit(solution)/shard_map/pallas_call | solution.py:364
  168.5 4.0 %shard_map.60 = (bf16[8,256,2048]{2,1,0:T(8,128)(2,1)}, bf16[256,4096]{1,0:T(8,128)(2,1)}) custom-call(bf16[8,256,2048]{2,1,0:T(8,128)(2,1)S(1)} %get-tuple-element.6.out, bf16[256,4096]{1,0:T(8,128)(2,1)S(1)} %get-tuple-element.7.attended), custom_call_target="tpu_custom_call" | custom-call | tf_op jit(solution)/shard_map/pallas_call | solution.py:402
Async XLA Ops:
  1.4 1.6 copy-start
  3.0 0.7 copy-start.1

commit v6 on v5

--- a/solution.py
+++ b/solution.py
@@ -260,7 +260,7 @@
         live = (second < counts[at]) & (slot - second * SUMLEN < BLOCK * live_blocks)
         bias[doc : doc + 1, :] = jnp.where(live, 0.0, NEGATIVE)
 
-    @pl.loop(1, 4)
+    @pl.loop(1, 5)
     def _(layer):
         z_send(layer)
 
@@ -285,13 +285,14 @@
             x * 2 + to_zh, to_core, qbuf.at[kv, src], keys.at[kv], keys.at[2 + kv], bias, s_ref, m_ref, l_ref, acc_ref
         )
 
-        @pl.when(t < 4)
-        def _():
-            z_send(t + 4)
-
-        @pl.when((t < 6) & (t != 2))
-        def _():
-            x_send(t + 2 - t // 3)
+        @pl.when((t == 0) | (t == 2) | (t == 3))
+        def _():
+            z_send(t - t // 2 + 5)
+            x_send(t - t // 2 + 2)
+
+        @pl.when((t == 4) | (t == 5))
+        def _():
+            x_send(t + 1)
 
         @pl.when(t == 3)
         def _():

time: 173 us -> 167 us (0.965)
  the two profiles are of different devices: /device:TPU:51 before, /device:TPU:30 now
where the time goes in v6:
time: 167 us; the launch traced here: 166 us
  Pallas kernels  162 us (97%)
  local copies, waits for them, and re-layouts  3.01 us (2%)
    pallas_call x1, Pallas kernels, relay(): pl.pallas_call(relay_kernel, out_shape=(jax.ShapeDtypeStruct((LAYERS, 256...  158 us
    pallas_call x1, Pallas kernels, settle(): pl.pallas_call(settle_kernel, out_shape=tuple((jax.ShapeDtypeStruct(a.sha...  4.04 us

profile of v6, /device:TPU:30, one launch (start us, length us, event | category | flops | bytes accessed | tf_op | source)
XLA Modules:
  0.0 166.1 jit_solution(9808853159110820124)
XLA Ops:
  0.6 0.8 copy.6.blocks_hbm
  1.4 0.0 copy-start
  1.4 1.6 copy-done
  3.0 0.0 copy-start.1
  3.0 0.7 copy-done.1
  3.6 158.4 %shard_map.59 = (bf16[8,256,2048]{2,1,0:T(8,128)(2,1)S(1)}, bf16[256,4096]{1,0:T(8,128)(2,1)S(1)}, bf16[8,2,2,2,512,128]{5,4,3,2,1,0:T(8,128)(2,1)}) custom-call(bf16[8,2,2,2,512,128]{5,4,3,2,1,0:T(8,128)(2,1)} %bitcast.7, bf16[256,4096]{1,0:T(8,128)(2,1)S(1)} %bitcast.6, s32[64]{0:T(128)S(1)} %copy-done.1, s32[64,2]{1,0:T(8,128)S(1)} %copy.6.blocks_hbm), custom_call_target="tpu_custom_call" | custom-call | tf_op jit(solution)/shard_map/pallas_call | solution.py:365
  162.0 4.0 %shard_map.60 = (bf16[8,256,2048]{2,1,0:T(8,128)(2,1)}, bf16[256,4096]{1,0:T(8,128)(2,1)}) custom-call(bf16[8,256,2048]{2,1,0:T(8,128)(2,1)S(1)} %get-tuple-element.6.out, bf16[256,4096]{1,0:T(8,128)(2,1)S(1)} %get-tuple-element.7.attended), custom_call_target="tpu_custom_call" | custom-call | tf_op jit(solution)/shard_map/pallas_call | solution.py:403
Async XLA Ops:
  1.4 1.6 copy-start
  3.0 0.7 copy-start.1

commit v7 on v6

--- a/solution.py
+++ b/solution.py
@@ -256,7 +256,7 @@
     second = slot // SUMLEN
     for doc in range(8):
         at = doc * 8 + d
-        live_blocks = jnp.where(second == 0, blocks[at, 0], blocks[at, 1])
+        live_blocks = jnp.where(second == 0, blocks[0, at], blocks[1, at])
         live = (second < counts[at]) & (slot - second * SUMLEN < BLOCK * live_blocks)
         bias[doc : doc + 1, :] = jnp.where(live, 0.0, NEGATIVE)
 
@@ -334,11 +334,6 @@
         for g in range(GROUP):
             for rel in (1, 2, 3):
                 q_copy(kv, g, rel).wait_send()
-                o_copy(kv, g, rel).wait()
-
-    for frm in range(4):
-        for rel in (1, 2, 3):
-            l_copy(frm, rel).wait()
 
     @pl.loop(1, LAYERS)
     def _(layer):
@@ -350,6 +345,15 @@
         for piece in range(4):
             for step in others:
                 x_copy(layer, step, piece).wait()
+
+    for kv in range(2):
+        for g in range(GROUP):
+            for rel in (1, 2, 3):
+                o_copy(kv, g, rel).wait()
+
+    for frm in range(4):
+        for rel in (1, 2, 3):
+            l_copy(frm, rel).wait()
 
 
 def relay(cache, queries, counts, blocks):
@@ -374,7 +378,7 @@
         scratch_shapes=[
             pltpu.VMEM((8, SEQD), f32),
             pltpu.SMEM((64,), jnp.int32),
-            pltpu.SMEM((64, SECTIONS), jnp.int32),
+            pltpu.SMEM((SECTIONS, 64), jnp.int32),
             pltpu.VMEM((4, 4, 2, SEQD, HD), bf),
             pltpu.VMEM((LAYERS - 1, 4, 4, 256, HD), bf),
             pltpu.VMEM((2, 4, rows, HD), bf),
@@ -386,7 +390,7 @@
         ]
         + [dma(shape) for shape in sems],
         compiler_params=pltpu.CompilerParams(collective_id=0, has_side_effects=True, vmem_limit_bytes=40 << 20),
-    )(cache.reshape(LAYERS, 2, 2, 2, SEQD, HD), queries, counts, blocks)
+    )(cache.reshape(LAYERS, 2, 2, 2, SEQD, HD), *(pltpu.with_memory_space_constraint(a, pltpu.HBM) for a in (queries, counts, blocks.T)))
 
 
 def settle_kernel(out, attended, out_to, attended_to, sems):

time: 167 us -> 164 us (0.982)
  local copies, waits for them, and re-layouts: 3.01 us -> 0 us
    unnamed x5 -> x0, local copies, waits for them, and re-layouts: 3.01 us -> none
where the time goes in v7:
time: 164 us; the launch traced here: 163 us
  Pallas kernels  163 us (99%)
    pallas_call x1, Pallas kernels, relay(): pl.pallas_call(relay_kernel, out_shape=(jax.ShapeDtypeStruct((LAYERS, 256...  158 us
    pallas_call x1, Pallas kernels, settle(): pl.pallas_call(settle_kernel, out_shape=tuple((jax.ShapeDtypeStruct(a.sha...  4.04 us

profile of v7, /device:TPU:30, one launch (start us, length us, event | category | flops | bytes accessed | tf_op | source)
XLA Modules:
  0.0 163.1 jit_solution(16523700968789195670)
XLA Ops:
  0.6 158.5 %shard_map.59 = (bf16[8,256,2048]{2,1,0:T(8,128)(2,1)S(1)}, bf16[256,4096]{1,0:T(8,128)(2,1)S(1)}, bf16[8,2,2,2,512,128]{5,4,3,2,1,0:T(8,128)(2,1)}) custom-call(bf16[8,2,2,2,512,128]{5,4,3,2,1,0:T(8,128)(2,1)} %bitcast.7, bf16[256,4096]{1,0:T(8,128)(2,1)} %bitcast.8, s32[64]{0:T(128)} %counts_hbm.1, s32[2,64]{1,0:T(2,128)} %bitcast.9), custom_call_target="tpu_custom_call" | custom-call | tf_op jit(solution)/shard_map/pallas_call | solution.py:369
  159.1 4.0 %shard_map.60 = (bf16[8,256,2048]{2,1,0:T(8,128)(2,1)}, bf16[256,4096]{1,0:T(8,128)(2,1)}) custom-call(bf16[8,256,2048]{2,1,0:T(8,128)(2,1)S(1)} %get-tuple-element.6.out, bf16[256,4096]{1,0:T(8,128)(2,1)S(1)} %get-tuple-element.7.attended), custom_call_target="tpu_custom_call" | custom-call | tf_op jit(solution)/shard_map/pallas_call | solution.py:407

commit v8 on v7

--- a/solution.py
+++ b/solution.py
@@ -78,7 +78,7 @@
 
 
 def relay_kernel(
-    cache, queries, counts_hbm, blocks_hbm, out, attended, ybuf, bias, counts, blocks, keys, zbuf, qbuf, obuf, s_ref, m_ref, l_ref, acc_ref,
+    cache, queries, counts_hbm, blocks_hbm, out, attended, ybuf, bias, counts, blocks, keys, zbuf, qbuf, obuf, qstack, s_ref, m_ref, l_ref, acc_ref,
     y0s, y0r, y0o, ys, yr, yo, z0s, z0r, z0o, zs, zr, gs, gr, xs, xr, ls, lr, qs, qr, os, rs, cs,
 ):
     d = lax.axis_index("doc")
@@ -151,19 +151,22 @@
         dst = out.at[0, :, head_cols(frm * 4 + chunk)]
         return remote(src, dst, ls.at[frm, rel], lr.at[frm, rel], peer_place(rel))
 
-    def q_copy(kv, g, rel):
+    def group_cols(k):
+        return pl.ds(pl.multiple_of(k * GROUP * HD, GROUP * HD), GROUP * HD)
+
+    def q_copy(kv, rel):
         to_zh, to_core = peer(rel)
-        src = queries.at[:, head_cols((kv * 4 + to_zh * 2 + to_core) * GROUP + g)]
-        dst = qbuf.at[kv, chunk, pl.ds(g * 256, 256)]
+        src = queries.at[:, group_cols(kv * 4 + to_zh * 2 + to_core)]
+        dst = qbuf.at[kv, chunk]
         if rel == 0:
-            return pltpu.make_async_copy(src, dst, qr.at[kv, g, 0])
-        return remote(src, dst, qs.at[kv, g, rel], qr.at[kv, g, rel], peer_place(rel))
-
-    def o_copy(kv, g, rel):
+            return pltpu.make_async_copy(src, dst, qr.at[kv, 0])
+        return remote(src, dst, qs.at[kv, rel], qr.at[kv, rel], peer_place(rel))
+
+    def o_copy(kv, rel):
         to_zh, to_core = peer(rel)
-        src = obuf.at[kv, to_zh * 2 + to_core, pl.ds(g * 256, 256)]
-        dst = attended.at[:, head_cols((kv * 4 + chunk) * GROUP + g)]
-        return remote(src, dst, os.at[kv, g, rel], rs.at[kv, g, rel], peer_place(rel))
+        src = obuf.at[kv, to_zh * 2 + to_core]
+        dst = attended.at[:, group_cols(kv * 4 + chunk)]
+        return remote(src, dst, os.at[kv, rel], rs.at[kv, rel], peer_place(rel))
 
     zorder = ((1, 0), (1, 1), (3, 0), (3, 1), (2, 0), (2, 1), (0, 1), (0, 0))
 
@@ -171,16 +174,16 @@
         to_z, to_core = lax.rem(z + step, 4), lax.rem(core + flip, 2)
         r = step * 2 + flip
         src = ybuf.at[layer, :, to_z // 2, lax.rem(to_z, 2), half_rows(to_core)]
-        dst = zbuf.at[layer - 1, pl.ds(zl * 2, 2), chunk]
+        dst = zbuf.at[layer - 1, pl.ds(zl * 2, 2), :, head_cols(chunk)]
         if r == 0:
             return pltpu.make_async_copy(src, dst, zr.at[layer - 1, 0])
         return remote(src, dst, zs.at[layer - 1, r], zr.at[layer - 1, r], place(x, y, to_z, to_core))
 
-    def x_copy(layer, step, piece):
+    def x_copy(layer, step):
         to = lax.rem(x + step, 4)
-        src = zbuf.at[layer - 1, to, piece]
-        dst = out.at[layer, :, head_cols(x * 4 + piece)]
-        return remote(src, dst, xs.at[layer - 1, step - 1, piece], xr.at[layer - 1, step - 1, piece], place(to, y, z, core))
+        src = zbuf.at[layer - 1, to]
+        dst = out.at[layer, :, group_cols(x)]
+        return remote(src, dst, xs.at[layer - 1, step - 1], xr.at[layer - 1, step - 1], place(to, y, z, core))
 
     def z_send(layer):
         y_wait(layer)
@@ -194,10 +197,8 @@
             else:
                 z_copy(layer, step, flip).wait_recv()
         for step in others:
-            for piece in range(4):
-                x_copy(layer, step, piece).start()
-        for piece in range(4):
-            out[layer, :, head_cols(x * 4 + piece)] = zbuf[layer - 1, x, piece]
+            x_copy(layer, step).start()
+        out[layer, :, group_cols(x)] = zbuf[layer - 1, x]
 
     barrier = pltpu.get_barrier_semaphore()
     peers = [place(x, lax.rem(y + step, 4), z, core) for step in others]
@@ -222,12 +223,11 @@
         for step in others + (0,):
             y_copy(layer, step).start()
 
-    def q_send(kv, g):
+    def q_send(kv):
         for rel in (3, 2, 1, 0):
-            q_copy(kv, g, rel).start()
-
-    for g in range(2):
-        q_send(0, g)
+            q_copy(kv, rel).start()
+
+    q_send(0)
 
     @pl.loop(0, ROUNDS + 1)
     def _(t):
@@ -244,11 +244,7 @@
             for step in others:
                 when_is(lax.rem(x + step, 4), range(4), lambda v: g_copy(t - 1, step, v + 1).start())
 
-        when_is(t, range(2), lambda v: q_send(0, 2 + v))
-        when_is(t, range(2, 4), lambda v: q_send(1, v - 2))
-
-    for g in range(2, GROUP):
-        q_send(1, g)
+        when_is(t, (2,), lambda v: q_send(1))
 
     for copy in tables:
         copy.wait()
@@ -278,12 +274,15 @@
         rel = 3 - t // 2
         kv = lax.rem(t, 2)
         to_zh, to_core = peer(rel)
+        pltpu.make_async_copy(queries.at[:, group_cols(0)], qbuf.at[kv, 0], qr.at[kv, rel]).wait()
+        src = to_zh * 2 + to_core
         for g in range(GROUP):
-            pltpu.make_async_copy(queries.at[:, head_cols(g)], qbuf.at[kv, 0, pl.ds(g * 256, 256)], qr.at[kv, g, rel]).wait()
-        src = to_zh * 2 + to_core
-        obuf[kv, src] = head_group(
-            x * 2 + to_zh, to_core, qbuf.at[kv, src], keys.at[kv], keys.at[2 + kv], bias, s_ref, m_ref, l_ref, acc_ref
+            qstack[g * 256 : (g + 1) * 256, :] = qbuf[kv, src, :, g * HD : (g + 1) * HD]
+        result = head_group(
+            x * 2 + to_zh, to_core, qstack, keys.at[kv], keys.at[2 + kv], bias, s_ref, m_ref, l_ref, acc_ref
         )
+        for g in range(GROUP):
+            obuf[kv, src, :, g * HD : (g + 1) * HD] = result[g * 256 : (g + 1) * 256]
 
         @pl.when((t == 0) | (t == 2) | (t == 3))
         def _():
@@ -298,18 +297,15 @@
         def _():
             for rel in (3, 2):
                 for kv in range(2):
-                    for g in range(GROUP):
-                        o_copy(kv, g, rel).start()
+                    o_copy(kv, rel).start()
 
         @pl.when((t == 4) | (t == 5))
         def _():
-            for g in range(GROUP):
-                o_copy(kv, g, 1).start()
+            o_copy(kv, 1).start()
 
         @pl.when(t >= 6)
         def _():
-            for g in range(GROUP):
-                attended[:, head_cols((kv * 4 + chunk) * GROUP + g)] = obuf[kv, chunk, pl.ds(g * 256, 256)]
+            attended[:, group_cols(kv * 4 + chunk)] = obuf[kv, chunk]
 
         @pl.when(t == 4)
         def _():
@@ -331,9 +327,8 @@
         z0_copy(u, 1).wait_send()
 
     for kv in range(2):
-        for g in range(GROUP):
-            for rel in (1, 2, 3):
-                q_copy(kv, g, rel).wait_send()
+        for rel in (1, 2, 3):
+            q_copy(kv, rel).wait_send()
 
     @pl.loop(1, LAYERS)
     def _(layer):
@@ -342,14 +337,12 @@
         for step, flip in zorder:
             if step * 2 + flip:
                 z_copy(layer, step, flip).wait_send()
-        for piece in range(4):
-            for step in others:
-                x_copy(layer, step, piece).wait()
+        for step in others:
+            x_copy(layer, step).wait()
 
     for kv in range(2):
-        for g in range(GROUP):
-            for rel in (1, 2, 3):
-                o_copy(kv, g, rel).wait()
+        for rel in (1, 2, 3):
+            o_copy(kv, rel).wait()
 
     for frm in range(4):
         for rel in (1, 2, 3):
@@ -364,7 +357,7 @@
     anyspace = pl.BlockSpec(memory_space=pl.ANY)
     sems = [
         (4, 3), (4, 3), (4,), (7, 3), (7, 3), (7,), (4,), (4,), (4,), (7, 8), (7, 8), (4, 3), (4, 3),
-        (7, 3, 4), (7, 3, 4), (4, 4), (4, 4), (2, 4, 4), (2, 4, 4), (2, 4, 4), (2, 4, 4), (2,),
+        (7, 3), (7, 3), (4, 4), (4, 4), (2, 4), (2, 4), (2, 4), (2, 4), (2,),
     ]
     return pl.pallas_call(
         relay_kernel,
@@ -380,9 +373,10 @@
             pltpu.SMEM((64,), jnp.int32),
             pltpu.SMEM((SECTIONS, 64), jnp.int32),
             pltpu.VMEM((4, 4, 2, SEQD, HD), bf),
-            pltpu.VMEM((LAYERS - 1, 4, 4, 256, HD), bf),
-            pltpu.VMEM((2, 4, rows, HD), bf),
-            pltpu.VMEM((2, 4, rows, HD), bf),
+            pltpu.VMEM((LAYERS - 1, 4, 256, 4 * HD), bf),
+            pltpu.VMEM((2, 4, 256, GROUP * HD), bf),
+            pltpu.VMEM((2, 4, 256, GROUP * HD), bf),
+            pltpu.VMEM((rows, HD), bf),
             pltpu.VMEM((8, rows, SEQD), f32),
             pltpu.VMEM((rows, 128), f32),
             pltpu.VMEM((rows, 128), f32),

time: 164 us -> 164 us (level)
  no operation moved by 1% of the time
where the time goes in v8:
time: 164 us; the launch traced here: 162 us
  Pallas kernels  162 us (99%)
    pallas_call x1, Pallas kernels, relay(): pl.pallas_call(relay_kernel, out_shape=(jax.ShapeDtypeStruct((LAYERS, 256...  158 us
    pallas_call x1, Pallas kernels, settle(): pl.pallas_call(settle_kernel, out_shape=tuple((jax.ShapeDtypeStruct(a.sha...  4.04 us

profile of v8, /device:TPU:30, one launch (start us, length us, event | category | flops | bytes accessed | tf_op | source)
XLA Modules:
  0.0 162.4 jit_solution(2708004445102191633)
XLA Ops:
  0.6 157.7 %shard_map.59 = (bf16[8,256,2048]{2,1,0:T(8,128)(2,1)S(1)}, bf16[256,4096]{1,0:T(8,128)(2,1)S(1)}, bf16[8,2,2,2,512,128]{5,4,3,2,1,0:T(8,128)(2,1)}) custom-call(bf16[8,2,2,2,512,128]{5,4,3,2,1,0:T(8,128)(2,1)} %bitcast.7, bf16[256,4096]{1,0:T(8,128)(2,1)} %bitcast.8, s32[64]{0:T(128)} %counts_hbm.1, s32[2,64]{1,0:T(2,128)} %bitcast.9), custom_call_target="tpu_custom_call" | custom-call | tf_op jit(solution)/shard_map/pallas_call | solution.py:362
  158.4 4.0 %shard_map.60 = (bf16[8,256,2048]{2,1,0:T(8,128)(2,1)}, bf16[256,4096]{1,0:T(8,128)(2,1)}) custom-call(bf16[8,256,2048]{2,1,0:T(8,128)(2,1)S(1)} %get-tuple-element.6.out, bf16[256,4096]{1,0:T(8,128)(2,1)S(1)} %get-tuple-element.7.attended), custom_call_target="tpu_custom_call" | custom-call | tf_op jit(solution)/shard_map/pallas_call | solution.py:401
